TPU v7x, 256 devices: a whole 4x4x8 slice. The times are simulated.
256 devices in a mesh: ta: 8 (over z_lo, x), ha: 4 (over y), wa: 8 (over z_hi, core).
Axes of the slice: x: 4, y: 4, z: 8 (z_hi: 4, z_lo: 2; z = z_hi * 2 + z_lo), core: 2. Of those that a mesh axis runs over, the one named last changes fastest.
Arguments:
- volume: bfloat16 [8, 128, 128, 128], P('ta', 'ha', 'wa'), may hold values from -6 to 6
- cotangent: bfloat16 [8, 128, 128, 128], P('ta', 'ha', 'wa'), may hold values from -6 to 6
- kernel_one: bfloat16 [3, 3, 3, 128, 128], replicated, may hold values from -0.109375 to 0.109375
- kernel_two: bfloat16 [3, 3, 3, 128, 128], replicated, may hold values from -0.109375 to 0.109375
Outputs:
- d_volume: bfloat16 [8, 128, 128, 128], P('ta', 'ha', 'wa')
- grad_one: float32 [3, 3, 3, 128, 128], replicated
- grad_two: float32 [3, 3, 3, 128, 128], replicated
All inputs are finite; a program needn't handle non-finite values.
Results may differ from a plain program's by a relative error of at most 0.0049.
Values may be sent and summed in bfloat16 or wider, within the bound.
A program may use at most 64 MiB of HBM per device.

v0:
```python
import jax
import jax.numpy as jnp
from jax import lax
from jax.sharding import PartitionSpec as P


def padded_2(cells, sides, width):
    for axis, dim in sides:
        count = lax.axis_size(axis)
        ends = count - 1
        head = lax.slice_in_dim(cells, 0, width, axis=dim)
        tail = lax.slice_in_dim(cells, cells.shape[dim] - width, cells.shape[dim], axis=dim)
        cells = jnp.concatenate(
            [
                lax.ppermute(tail, axis, [(i, (i + 1) % count) for i in range(ends)]),
                cells,
                lax.ppermute(head, axis, [((i + 1) % count, i) for i in range(ends)]),
            ],
            axis=dim,
        )
    return cells


def flip_swap(kernel):
    return jnp.swapaxes(kernel[::-1, ::-1, ::-1], 3, 4)


def window_rows(padded, offset_t, offset_h):
    frames = padded.shape[0] - 2
    height = padded.shape[1] - 2
    width = padded.shape[2] - 2
    chans = padded.shape[3]
    pieces = [
        padded[offset_t : offset_t + frames, offset_h : offset_h + height, shift : shift + width]
        for shift in range(3)
    ]
    return jnp.concatenate(pieces, axis=-1).reshape(-1, 3 * chans)


def conv_local(padded, kernel):
    frames = padded.shape[0] - 2
    height = padded.shape[1] - 2
    width = padded.shape[2] - 2
    chans = padded.shape[3]
    total = jnp.zeros((frames * height * width, chans), jnp.float32)
    for offset_t in range(3):
        for offset_h in range(3):
            rows = window_rows(padded, offset_t, offset_h)
            total = total + jnp.dot(
                rows,
                kernel[offset_t, offset_h].reshape(3 * chans, chans),
                preferred_element_type=jnp.float32,
            )
    return total.reshape(frames, height, width, chans)


def kernel_local(padded, other):
    chans = padded.shape[3]
    right = other.reshape(-1, chans)
    blocks = []
    for offset_t in range(3):
        for offset_h in range(3):
            rows = window_rows(padded, offset_t, offset_h)
            product = lax.dot_general(
                rows, right, (((0,), (0,)), ((), ())), preferred_element_type=jnp.float32
            )
            blocks.append(product.reshape(3, chans, chans))
    return jnp.stack(blocks).reshape(3, 3, 3, chans, chans)


def body(volume, cotangent, kernel_one, kernel_two):
    stacked = jnp.stack((volume, cotangent))
    padded_both = padded_2(stacked, (("ta", 1), ("ha", 2), ("wa", 3)), 1)
    volume_pad = padded_both[0]
    cotangent_pad = padded_both[1]
    pre = conv_local(volume_pad, kernel_one)
    sig = jax.nn.sigmoid(pre)
    hidden = (pre * sig).astype(jnp.bfloat16)
    d_hidden = conv_local(cotangent_pad, flip_swap(kernel_two))
    d_pre = (d_hidden * sig * (1.0 + pre * (1.0 - sig))).astype(jnp.bfloat16)
    total_cells = (
        volume.shape[0]
        * volume.shape[1]
        * volume.shape[2]
        * lax.axis_size("ta")
        * lax.axis_size("ha")
        * lax.axis_size("wa")
    )
    scale = 1.0 / jnp.sqrt(jnp.float32(total_cells))
    part_two = flip_swap(kernel_local(cotangent_pad, hidden))
    d_pre_pad = padded_2(d_pre, (("ta", 0), ("ha", 1), ("wa", 2)), 1)
    d_volume = conv_local(d_pre_pad, flip_swap(kernel_one)).astype(jnp.bfloat16)
    part_one = kernel_local(volume_pad, d_pre)
    summed_one, summed_two = lax.psum((part_one, part_two), ("ta", "ha", "wa"))
    return (d_volume, summed_one * scale, summed_two * scale)


def solution(mesh):
    in_specs = (P("ta", "ha", "wa", None), P("ta", "ha", "wa", None), P(), P())
    out_specs = (P("ta", "ha", "wa", None), P(), P())
    return jax.shard_map(body, mesh=mesh, in_specs=in_specs, out_specs=out_specs, check_vma=False)
```

profile of v0, /device:TPU:1, one launch (start us, length us, event | category | flops | bytes accessed | tf_op | source)
XLA Modules:
  0.0 404.6 jit_solution(5798208875748316592)
XLA Ops:
  9.0 3.9 collective-permute-start
  14.2 2.2 fusion.57
  22.0 3.2 collective-permute-start.2
  26.6 3.2 collective-permute-done.3
  29.9 8.0 %collective-permute-start.4 = (bf16[2,3,34,1,128]{4,3,2,1,0:T(2,128)(2,1)S(1)}, bf16[2,3,34,1,128]{4,3,2,1,0:T(2,128)(2,1)S(1)}, u32[]{:S(2)}, u32[]{:S(2)}) collective-permute-start(bf16[2,3,34,1,128]{4,3,2,1,0:T(2,128)(2,1)S(1)} %get-tuple-element.34), channel_id=1, source_target_pairs={{0,1},{1,2},{2,3},{3,4},{4,5},{5,6},{6,7},{8,9},{9,10},{10,11},{11... | collective-permute-start | bytes 156680 | tf_op jit(solution)/shard_map/ppermute | solution.py:15
  37.9 1.9 collective-permute-start.5
  40.8 4.0 %collective-permute-done.5 = bf16[2,3,34,1,128]{4,3,2,1,0:T(2,128)(2,1)S(1)} collective-permute-done((bf16[2,3,34,1,128]{4,3,2,1,0:T(2,128)(2,1)S(1)}, bf16[2,3,34,1,128]{4,3,2,1,0:T(2,128)(2,1)S(1)}, u32[]{:S(2)}, u32[]{:S(2)}) %collective-permute-start.5) | collective-permute-done | bytes 52256 | tf_op jit(solution)/shard_map/ppermute | solution.py:17
  68.5 2.2 pad_maximum_fusion.32
  70.7 1.9 copy.31
  72.6 1.9 copy.32
  74.5 2.2 pad_maximum_fusion.34
  76.7 1.9 copy.33
  78.6 1.9 copy.34
  80.5 2.2 pad_maximum_fusion.36
  82.7 1.9 copy.35
  84.6 2.0 copy.36
  93.8 3.2 collective-permute-start.6
  103.5 3.2 collective-permute-start.8
  109.5 2.4 copy.46
  112.0 3.7 collective-permute-start.10
  115.7 1.9 collective-permute-start.11
  119.1 5.5 %collective-permute-done.11 = bf16[3,34,1,128]{3,2,1,0:T(2,128)(2,1)S(1)} collective-permute-done((bf16[3,34,1,128]{3,2,1,0:T(2,128)(2,1)S(1)}, bf16[3,34,1,128]{3,2,1,0:T(2,128)(2,1)S(1)}, u32[]{:S(2)}, u32[]{:S(2)}) %collective-permute-start.11) | collective-permute-done | bytes 26144 | tf_op jit(solution)/shard_map/ppermute | solution.py:17
  130.5 262.7 %all-reduce.3.cloned.1.call-done = (f32[3,3,3,128,128]{4,3,2,1,0:T(8,128)}, f32[3,3,3,128,128]{4,3,2,1,0:T(8,128)}) async-done(((f32[3,3,3,128,128]{4,3,2,1,0:T(8,128)}, f32[3,3,3,128,128]{4,3,2,1,0:T(8,128)}), (f32[3,3,3,128,128]{4,3,2,1,0:T(8,128)}, f32[3,3,3,128,128]{4,3,2,1,0:T(8,128)})) %all-reduce.3.cloned.1.call-update) | async-done | bytes 3538960 | tf_op jit(solution)/shard_map/psum | solution.py:94
  393.3 3.1 broadcast_multiply_fusion
  (235 shorter events, 58.8 us)
Async XLA Ops:
  7.2 9.3 %copy-start.33 = (bf16[3,3,3,128,128]{4,3,2,1,0:T(8,128)(2,1)S(1)}, bf16[3,3,3,128,128]{4,3,2,1,0:T(8,128)(2,1)}, u32[]{:S(2)}) copy-start(bf16[3,3,3,128,128]{4,3,2,1,0:T(8,128)(2,1)} %param.7) | copy-start | bytes 2654212
  7.2 386.1 %all-reduce.3.cloned.1.call-start = ((), (), s32[]{:S(2)}) async-start(), calls=%async_computation | async-start | bytes 7077888 | tf_op jit(solution)/shard_map/psum | solution.py:94
  9.0 11.4 %collective-permute-start = (bf16[2,1,32,16,128]{4,3,2,1,0:T(8,128)(2,1)}, bf16[2,1,32,16,128]{4,3,2,1,0:T(8,128)(2,1)S(1)}, u32[]{:S(2)}, u32[]{:S(2)}) collective-permute-start(bf16[2,1,32,16,128]{4,3,2,1,0:T(8,128)(2,1)} %pad_maximum_fusion.40), channel_id=1, source_target_pairs={{0,32},{32,64},{64,96},{96,128},{128,160},{160,192},{192,224},{1,3... | collective-permute-start | bytes 786440 | tf_op jit(solution)/shard_map/ppermute | solution.py:15
  12.9 9.0 %collective-permute-start.1 = (bf16[2,1,32,16,128]{4,3,2,1,0:T(8,128)(2,1)}, bf16[2,1,32,16,128]{4,3,2,1,0:T(8,128)(2,1)S(1)}, u32[]{:S(2)}, u32[]{:S(2)}) collective-permute-start(bf16[2,1,32,16,128]{4,3,2,1,0:T(8,128)(2,1)} %pad_maximum_fusion.40), channel_id=1, source_target_pairs={{32,0},{64,32},{96,64},{128,96},{160,128},{192,160},{224,192},{33,... | collective-permute-start | bytes 786440 | tf_op jit(solution)/shard_map/ppermute | solution.py:17
  18.0 4.0 copy-start.10
  22.0 4.6 %collective-permute-start.2 = (bf16[2,3,1,16,128]{4,3,2,1,0:T(8,128)(2,1)S(1)}, bf16[2,3,1,16,128]{4,3,2,1,0:T(8,128)(2,1)S(1)}, u32[]{:S(2)}, u32[]{:S(2)}) collective-permute-start(bf16[2,3,1,16,128]{4,3,2,1,0:T(8,128)(2,1)S(1)} %get-tuple-element.36), channel_id=1, source_target_pairs={{0,8},{8,16},{16,24},{1,9},{9,17},{17,25},{2,10},{10,18},{18,26},{... | collective-permute-start | bytes 73736 | tf_op jit(solution)/shard_map/ppermute | solution.py:15
  25.2 4.6 %collective-permute-start.3 = (bf16[2,3,1,16,128]{4,3,2,1,0:T(8,128)(2,1)S(1)}, bf16[2,3,1,16,128]{4,3,2,1,0:T(8,128)(2,1)S(1)}, u32[]{:S(2)}, u32[]{:S(2)}) collective-permute-start(bf16[2,3,1,16,128]{4,3,2,1,0:T(8,128)(2,1)S(1)} %get-tuple-element.37), channel_id=1, source_target_pairs={{8,0},{16,8},{24,16},{9,1},{17,9},{25,17},{10,2},{18,10},{26,18},{... | collective-permute-start | bytes 73736 | tf_op jit(solution)/shard_map/ppermute | solution.py:17
  29.9 10.9 %collective-permute-start.4 = (bf16[2,3,34,1,128]{4,3,2,1,0:T(2,128)(2,1)S(1)}, bf16[2,3,34,1,128]{4,3,2,1,0:T(2,128)(2,1)S(1)}, u32[]{:S(2)}, u32[]{:S(2)}) collective-permute-start(bf16[2,3,34,1,128]{4,3,2,1,0:T(2,128)(2,1)S(1)} %get-tuple-element.34), channel_id=1, source_target_pairs={{0,1},{1,2},{2,3},{3,4},{4,5},{5,6},{6,7},{8,9},{9,10},{10,11},{11... | collective-permute-start | bytes 156680 | tf_op jit(solution)/shard_map/ppermute | solution.py:15
  37.9 6.9 %collective-permute-start.5 = (bf16[2,3,34,1,128]{4,3,2,1,0:T(2,128)(2,1)S(1)}, bf16[2,3,34,1,128]{4,3,2,1,0:T(2,128)(2,1)S(1)}, u32[]{:S(2)}, u32[]{:S(2)}) collective-permute-start(bf16[2,3,34,1,128]{4,3,2,1,0:T(2,128)(2,1)S(1)} %get-tuple-element.35), channel_id=1, source_target_pairs={{1,0},{2,1},{3,2},{4,3},{5,4},{6,5},{7,6},{9,8},{10,9},{11,10},{12... | collective-permute-start | bytes 156680 | tf_op jit(solution)/shard_map/ppermute | solution.py:17
  49.6 5.8 %copy-start.34 = (bf16[1,32,16,128]{3,2,1,0:T(8,128)(2,1)S(1)}, bf16[1,32,16,128]{3,2,1,0:T(8,128)(2,1)}, u32[]{:S(2)}) copy-start(bf16[1,32,16,128]{3,2,1,0:T(8,128)(2,1)} %get-tuple-element.77) | copy-start | bytes 393220
  49.6 5.8 %copy-start.35 = (bf16[1,32,16,128]{3,2,1,0:T(8,128)(2,1)S(1)}, bf16[1,32,16,128]{3,2,1,0:T(8,128)(2,1)}, u32[]{:S(2)}) copy-start(bf16[1,32,16,128]{3,2,1,0:T(8,128)(2,1)} %get-tuple-element.78) | copy-start | bytes 393220
  49.6 5.7 %copy-start.36 = (bf16[1,32,16,128]{3,2,1,0:T(8,128)(2,1)S(1)}, bf16[1,32,16,128]{3,2,1,0:T(8,128)(2,1)}, u32[]{:S(2)}) copy-start(bf16[1,32,16,128]{3,2,1,0:T(8,128)(2,1)} %get-tuple-element.79) | copy-start | bytes 393220
  93.0 5.6 %copy-start.14 = (bf16[512,384]{0,1:T(8,128)(2,1)S(1)}, bf16[512,384]{0,1:T(8,128)(2,1)}, u32[]{:S(2)}) copy-start(bf16[512,384]{0,1:T(8,128)(2,1)} %copy.37) | copy-start | bytes 1179652
  93.3 5.6 %copy-start.15 = (bf16[512,384]{0,1:T(8,128)(2,1)S(1)}, bf16[512,384]{0,1:T(8,128)(2,1)}, u32[]{:S(2)}) copy-start(bf16[512,384]{0,1:T(8,128)(2,1)} %copy.38) | copy-start | bytes 1179652
  93.4 5.8 %copy-start.16 = (bf16[512,384]{0,1:T(8,128)(2,1)S(1)}, bf16[512,384]{0,1:T(8,128)(2,1)}, u32[]{:S(2)}) copy-start(bf16[512,384]{0,1:T(8,128)(2,1)} %copy.39) | copy-start | bytes 1179652
  93.7 5.7 %copy-start.18 = (bf16[512,384]{0,1:T(8,128)(2,1)S(1)}, bf16[512,384]{0,1:T(8,128)(2,1)}, u32[]{:S(2)}) copy-start(bf16[512,384]{0,1:T(8,128)(2,1)} %copy.40) | copy-start | bytes 1179652
  93.7 6.0 %copy-start.17 = (bf16[512,384]{0,1:T(8,128)(2,1)S(1)}, bf16[512,384]{0,1:T(8,128)(2,1)}, u32[]{:S(2)}) copy-start(bf16[512,384]{0,1:T(8,128)(2,1)} %copy.41) | copy-start | bytes 1179652
  93.8 9.6 %collective-permute-start.6 = (bf16[1,32,16,128]{3,2,1,0:T(8,128)(2,1)S(1)}, bf16[1,32,16,128]{3,2,1,0:T(8,128)(2,1)S(1)}, u32[]{:S(2)}, u32[]{:S(2)}) collective-permute-start(bf16[1,32,16,128]{3,2,1,0:T(8,128)(2,1)S(1)} %multiply_convert_fusion.2), channel_id=1, source_target_pairs={{0,32},{32,64},{64,96},{96,128},{128,160},{160,192},{192,224},{1,3... | collective-permute-start | bytes 393224 | tf_op jit(solution)/shard_map/ppermute | solution.py:15
  97.1 6.4 %collective-permute-start.7 = (bf16[1,32,16,128]{3,2,1,0:T(8,128)(2,1)S(1)}, bf16[1,32,16,128]{3,2,1,0:T(8,128)(2,1)S(1)}, u32[]{:S(2)}, u32[]{:S(2)}) collective-permute-start(bf16[1,32,16,128]{3,2,1,0:T(8,128)(2,1)S(1)} %multiply_convert_fusion.2), channel_id=1, source_target_pairs={{32,0},{64,32},{96,64},{128,96},{160,128},{192,160},{224,192},{33,... | collective-permute-start | bytes 393224 | tf_op jit(solution)/shard_map/ppermute | solution.py:17
  102.3 5.7 %copy-start.25 = (bf16[512,384]{0,1:T(8,128)(2,1)S(1)}, bf16[512,384]{0,1:T(8,128)(2,1)}, u32[]{:S(2)}) copy-start(bf16[512,384]{0,1:T(8,128)(2,1)} %copy.36) | copy-start | bytes 1179652
  103.5 8.4 %collective-permute-start.8 = (bf16[3,1,16,128]{3,2,1,0:T(8,128)(2,1)S(1)}, bf16[3,1,16,128]{3,2,1,0:T(8,128)(2,1)S(1)}, u32[]{:S(2)}, u32[]{:S(2)}) collective-permute-start(bf16[3,1,16,128]{3,2,1,0:T(8,128)(2,1)S(1)} %get-tuple-element.121), channel_id=1, source_target_pairs={{0,8},{8,16},{16,24},{1,9},{9,17},{17,25},{2,10},{10,18},{18,26},{... | collective-permute-start | bytes 36872 | tf_op jit(solution)/shard_map/ppermute | solution.py:15
  106.7 5.2 %collective-permute-start.9 = (bf16[3,1,16,128]{3,2,1,0:T(8,128)(2,1)S(1)}, bf16[3,1,16,128]{3,2,1,0:T(8,128)(2,1)S(1)}, u32[]{:S(2)}, u32[]{:S(2)}) collective-permute-start(bf16[3,1,16,128]{3,2,1,0:T(8,128)(2,1)S(1)} %get-tuple-element.120), channel_id=1, source_target_pairs={{8,0},{16,8},{24,16},{9,1},{17,9},{25,17},{10,2},{18,10},{26,18},{... | collective-permute-start | bytes 36872 | tf_op jit(solution)/shard_map/ppermute | solution.py:17
  112.0 7.0 %collective-permute-start.10 = (bf16[3,34,1,128]{3,2,1,0:T(2,128)(2,1)S(1)}, bf16[3,34,1,128]{3,2,1,0:T(2,128)(2,1)S(1)}, u32[]{:S(2)}, u32[]{:S(2)}) collective-permute-start(bf16[3,34,1,128]{3,2,1,0:T(2,128)(2,1)S(1)} %get-tuple-element.112), channel_id=1, source_target_pairs={{0,1},{1,2},{2,3},{3,4},{4,5},{5,6},{6,7},{8,9},{9,10},{10,11},{11... | collective-permute-start | bytes 78344 | tf_op jit(solution)/shard_map/ppermute | solution.py:15
  115.7 8.9 %collective-permute-start.11 = (bf16[3,34,1,128]{3,2,1,0:T(2,128)(2,1)S(1)}, bf16[3,34,1,128]{3,2,1,0:T(2,128)(2,1)S(1)}, u32[]{:S(2)}, u32[]{:S(2)}) collective-permute-start(bf16[3,34,1,128]{3,2,1,0:T(2,128)(2,1)S(1)} %get-tuple-element.113), channel_id=1, source_target_pairs={{1,0},{2,1},{3,2},{4,3},{5,4},{6,5},{7,6},{9,8},{10,9},{11,10},{12... | collective-permute-start | bytes 78344 | tf_op jit(solution)/shard_map/ppermute | solution.py:17
  (53 other events, 83.5 us)
Sparse Core Ops, SparseCore 0:
  119.2 274.0 all-reduce.2
where the time goes:
time: 407 us; the launch traced here: 405 us
  waiting for transfers between devices  277 us (68%)
  local copies, waits for them, and re-layouts  41.2 us (10%)
  starting transfers between devices  34.5 us (8%)
  other arithmetic  18.7 us (5%)
  matrix products  17.8 us (4%)
  between operations  15.4 us (4%)
    psum x1, waiting for transfers between devices, body(): summed_one, summed_two = lax.psum((part_one, part_two), ('ta', 'ha', 'wa'))  263 us
    ppermute x6, starting transfers between devices, padded_2(): lax.ppermute(tail, axis, [(i, (i + 1) % count) for i in range(ends)])  25.3 us
    reshape x18, local copies, waits for them, and re-layouts, window_rows(): return jnp.concatenate(pieces, axis=-1).reshape(-1, 3 * chans)  22.8 us
    ppermute x6, waiting for transfers between devices, padded_2(): lax.ppermute(head, axis, [((i + 1) % count, i) for i in range(ends)])  14.3 us
    dot_general x27, matrix products, conv_local(): jnp.dot(rows, kernel[offset_t, offset_h].reshape(3 * chans, chans), prefe...  13.1 us
    concatenate x16, other arithmetic, window_rows(): return jnp.concatenate(pieces, axis=-1).reshape(-1, 3 * chans)  10.8 us
    ppermute x6, starting transfers between devices, padded_2(): lax.ppermute(head, axis, [((i + 1) % count, i) for i in range(ends)])  9.19 us
  transfers between devices with their start and end apart: 13, of which 5 were waited for; matrix products, arithmetic and copies ran while one was open for 5% of the time, Pallas kernels for 0%

commit v1 on v0

--- a/solution.py
+++ b/solution.py
@@ -1,7 +1,15 @@
+import functools
+
 import jax
 import jax.numpy as jnp
 from jax import lax
+from jax.experimental import pallas as pl
+from jax.experimental.pallas import tpu as pltpu
 from jax.sharding import PartitionSpec as P
+
+MESH = pl.DeviceIdType.MESH
+F32 = jnp.float32
+BF16 = jnp.bfloat16
 
 
 def padded_2(cells, sides, width):
@@ -66,6 +74,279 @@
             )
             blocks.append(product.reshape(3, chans, chans))
     return jnp.stack(blocks).reshape(3, 3, 3, chans, chans)
+
+
+class Place:
+    def __init__(self):
+        self.ta = lax.axis_index("ta")
+        self.ha = lax.axis_index("ha")
+        self.wa = lax.axis_index("wa")
+        self.core = lax.rem(self.wa, 2)
+        self.x = lax.rem(self.ta, 4)
+        self.y = self.ha
+        self.z = (self.wa // 2) * 2 + self.ta // 4
+
+    def peer_x(self, off):
+        to = lax.rem(self.x + off, 4)
+        return to, (self.ta - self.x + to, self.ha, self.wa)
+
+    def peer_y(self, off):
+        to = lax.rem(self.y + off, 4)
+        return to, (self.ta, to, self.wa)
+
+    def peer_z(self, off):
+        to = lax.rem(self.z + off, 8)
+        return to, (lax.rem(to, 2) * 4 + self.x, self.ha, (to // 2) * 2 + self.core)
+
+    def twin(self):
+        return (self.ta, self.ha, self.wa + 1 - 2 * self.core)
+
+
+def send(src, dst, send_sem, recv_sem, device):
+    pltpu.make_async_remote_copy(
+        src_ref=src, dst_ref=dst, send_sem=send_sem, recv_sem=recv_sem,
+        device_id=device, device_id_type=MESH,
+    ).start()
+
+
+def wait_bytes(ref, sem):
+    pltpu.make_async_copy(ref, ref, sem).wait()
+
+
+PHASES = 8
+
+
+class Reduce:
+    def __init__(self, place, part, full, land0, sums, land1, tops, land2, thirds, land3, lasts, sends, recvs):
+        self.at = place
+        self.part, self.full = part, full
+        self.land0, self.sums, self.land1 = land0, sums, land1
+        self.tops, self.land2 = tops, land2
+        self.thirds, self.land3, self.lasts = thirds, land3, lasts
+        self.sends, self.recvs = sends, recvs
+
+    def first(self, s, off):
+        return self.at.peer_x(off) if s == 0 else self.at.peer_y(off)
+
+    def second(self, s, off):
+        return self.at.peer_y(off) if s == 0 else self.at.peer_x(off)
+
+    def mine(self, s):
+        return (self.at.x, self.at.y) if s == 0 else (self.at.y, self.at.x)
+
+    def pair_send(self):
+        other = 4 - 4 * self.at.core
+        for s in range(2):
+            send(
+                self.part.at[pl.ds(other, 4), pl.ds(16 * s, 14)],
+                self.land0.at[s],
+                self.sends.at[0, s], self.recvs.at[0, s], self.at.twin(),
+            )
+
+    def pair_sum(self, s):
+        own = 4 * self.at.core
+        wait_bytes(self.land0.at[s], self.recvs.at[0, s])
+
+        def step(i, _):
+            total = self.part[own + i, pl.ds(16 * s, 14)].astype(F32) + self.land0[s, i].astype(F32)
+            self.sums[s, i] = total.astype(BF16)
+            return 0
+
+        lax.fori_loop(0, 4, step, 0)
+
+    def first_send(self, s):
+        for off in range(1, 4):
+            to, device = self.first(s, off)
+            send(
+                self.sums.at[s, to], self.land1.at[s, off - 1],
+                self.sends.at[1, s], self.recvs.at[1, s], device,
+            )
+
+    def first_sum(self, s):
+        me, _ = self.mine(s)
+        wait_bytes(self.land1.at[s], self.recvs.at[1, s])
+        total = self.sums[s, me].astype(F32)
+        for j in range(3):
+            total = total + self.land1[s, j].astype(F32)
+        self.tops[s, pl.ds(0, 14)] = total.astype(BF16)
+        self.tops[s, pl.ds(14, 2)] = jnp.zeros((2, 16, 128), BF16)
+
+    def second_send(self, s):
+        for off in range(1, 4):
+            to, device = self.second(s, off)
+            send(
+                self.tops.at[s, pl.ds(4 * to, 4)], self.land2.at[s, off - 1],
+                self.sends.at[2, s], self.recvs.at[2, s], device,
+            )
+
+    def second_sum(self, s):
+        _, me = self.mine(s)
+        wait_bytes(self.land2.at[s], self.recvs.at[2, s])
+        total = self.tops[s, pl.ds(4 * me, 4)].astype(F32)
+        for j in range(3):
+            total = total + self.land2[s, j].astype(F32)
+        self.thirds[s] = total.reshape(8, 8, 128)
+
+    def third_send(self, s):
+        for off in range(1, 8):
+            to, device = self.at.peer_z(off)
+            send(
+                self.thirds.at[s, to], self.land3.at[s, off - 1],
+                self.sends.at[3, s], self.recvs.at[3, s], device,
+            )
+
+    def third_sum(self, s):
+        wait_bytes(self.land3.at[s], self.recvs.at[3, s])
+        total = self.thirds[s, self.at.z]
+        for j in range(7):
+            total = total + self.land3[s, j]
+        self.lasts[s, self.at.z] = total
+
+    def third_gather(self, s):
+        for off in range(1, 8):
+            _, device = self.at.peer_z(off)
+            send(
+                self.lasts.at[s, self.at.z], self.lasts.at[s, self.at.z],
+                self.sends.at[4, s], self.recvs.at[4, s], device,
+            )
+
+    def second_gather(self, s):
+        me, me2 = self.mine(s)
+        wait_bytes(self.lasts.at[s, pl.ds(0, 7)], self.recvs.at[4, s])
+        row = 4 * self.at.core + me
+        spot = pl.ds(16 * s + 4 * me2, 4)
+        self.full[row, spot] = self.lasts[s].reshape(4, 16, 128).astype(BF16)
+        for off in range(1, 4):
+            _, device = self.second(s, off)
+            send(
+                self.full.at[row, spot], self.full.at[row, spot],
+                self.sends.at[5, s], self.recvs.at[5, s], device,
+            )
+
+    def first_gather(self, s):
+        me, me2 = self.mine(s)
+        wait_bytes(self.full.at[0, pl.ds(0, 12)], self.recvs.at[5, s])
+        row = 4 * self.at.core + me
+        spot = pl.ds(16 * s, 14)
+        for off in range(1, 4):
+            _, device = self.first(s, off)
+            send(
+                self.full.at[row, spot], self.full.at[row, spot],
+                self.sends.at[6, s], self.recvs.at[6, s], device,
+            )
+
+    def pair_gather(self, s):
+        wait_bytes(self.full.at[pl.ds(0, 3), pl.ds(0, 14)], self.recvs.at[6, s])
+        rows = pl.ds(4 * self.at.core, 4)
+        spot = pl.ds(16 * s, 14)
+        send(
+            self.full.at[rows, spot], self.full.at[rows, spot],
+            self.sends.at[7, s], self.recvs.at[7, s], self.at.twin(),
+        )
+
+    def finish(self, s):
+        wait_bytes(self.full.at[pl.ds(0, 4), pl.ds(0, 14)], self.recvs.at[7, s])
+
+    def drain(self, s):
+        wait_bytes(self.land0.at[s], self.sends.at[0, s])
+        wait_bytes(self.land1.at[s], self.sends.at[1, s])
+        wait_bytes(self.land2.at[s], self.sends.at[2, s])
+        wait_bytes(self.land3.at[s], self.sends.at[3, s])
+        wait_bytes(self.lasts.at[s, pl.ds(0, 7)], self.sends.at[4, s])
+        wait_bytes(self.full.at[0, pl.ds(0, 12)], self.sends.at[5, s])
+        wait_bytes(self.full.at[pl.ds(0, 3), pl.ds(0, 14)], self.sends.at[6, s])
+        wait_bytes(self.full.at[pl.ds(0, 4), pl.ds(0, 14)], self.sends.at[7, s])
+
+
+REDUCE_SCRATCH = [
+    pltpu.VMEM((2, 4, 14, 16, 128), BF16),
+    pltpu.VMEM((2, 4, 14, 16, 128), BF16),
+    pltpu.VMEM((2, 3, 14, 16, 128), BF16),
+    pltpu.VMEM((2, 16, 16, 128), BF16),
+    pltpu.VMEM((2, 3, 4, 16, 128), BF16),
+    pltpu.VMEM((2, 8, 8, 128), F32),
+    pltpu.VMEM((2, 7, 8, 128), F32),
+    pltpu.VMEM((2, 8, 8, 128), F32),
+    pltpu.SemaphoreType.DMA((PHASES, 2)),
+    pltpu.SemaphoreType.DMA((PHASES, 2)),
+]
+
+
+def enter(place, others):
+    barrier = pltpu.get_barrier_semaphore()
+    for device in others:
+        pl.semaphore_signal(barrier, inc=1, device_id=device, device_id_type=MESH)
+    pl.semaphore_wait(barrier, len(others))
+
+
+def reduce_peers(place):
+    peers = [place.twin()]
+    peers += [place.peer_x(off)[1] for off in range(1, 4)]
+    peers += [place.peer_y(off)[1] for off in range(1, 4)]
+    peers += [place.peer_z(off)[1] for off in range(1, 8)]
+    return peers
+
+
+def reduce_kernel(one, two, full_one, full_two, *scratch):
+    place = Place()
+    enter(place, reduce_peers(place))
+    size = len(REDUCE_SCRATCH)
+    grads = [
+        Reduce(place, two, full_two, *scratch[:size]),
+        Reduce(place, one, full_one, *scratch[size:]),
+    ]
+    todo = [(g, s) for g in grads for s in range(2)]
+    for g in grads:
+        g.pair_send()
+    for g, s in todo:
+        g.pair_sum(s)
+        g.first_send(s)
+    for g, s in todo:
+        g.first_sum(s)
+        g.second_send(s)
+    for g, s in todo:
+        g.second_sum(s)
+        g.third_send(s)
+    for g, s in todo:
+        g.third_sum(s)
+        g.third_gather(s)
+    for g, s in todo:
+        g.second_gather(s)
+    for g, s in todo:
+        g.first_gather(s)
+    for g, s in todo:
+        g.pair_gather(s)
+    for g, s in todo:
+        g.finish(s)
+    for g, s in todo:
+        g.drain(s)
+
+
+def to_slots(grad):
+    tiles = grad.reshape(27, 8, 16, 128).astype(BF16)
+    tiles = jnp.swapaxes(tiles, 0, 1)
+    hole = jnp.zeros((8, 2, 16, 128), BF16)
+    last = jnp.zeros((8, 3, 16, 128), BF16)
+    return jnp.concatenate([tiles[:, :14], hole, tiles[:, 14:], last], axis=1)
+
+
+def from_slots(full, scale):
+    tiles = jnp.concatenate([full[:, :14], full[:, 16:29]], axis=1)
+    tiles = jnp.swapaxes(tiles, 0, 1).astype(F32) * scale
+    return tiles.reshape(3, 3, 3, 128, 128)
+
+
+def all_sum(one, two, scale):
+    shape = jax.ShapeDtypeStruct((8, 32, 16, 128), BF16)
+    full_one, full_two = pl.pallas_call(
+        reduce_kernel,
+        out_shape=(shape, shape),
+        in_specs=[pl.BlockSpec(memory_space=pltpu.VMEM)] * 2,
+        out_specs=[pl.BlockSpec(memory_space=pltpu.VMEM)] * 2,
+        scratch_shapes=REDUCE_SCRATCH + REDUCE_SCRATCH,
+        compiler_params=pltpu.CompilerParams(collective_id=0, has_side_effects=True),
+    )(to_slots(one), to_slots(two))
+    return from_slots(full_one, scale), from_slots(full_two, scale)
 
 
 def body(volume, cotangent, kernel_one, kernel_two):
@@ -91,8 +372,8 @@
     d_pre_pad = padded_2(d_pre, (("ta", 0), ("ha", 1), ("wa", 2)), 1)
     d_volume = conv_local(d_pre_pad, flip_swap(kernel_one)).astype(jnp.bfloat16)
     part_one = kernel_local(volume_pad, d_pre)
-    summed_one, summed_two = lax.psum((part_one, part_two), ("ta", "ha", "wa"))
-    return (d_volume, summed_one * scale, summed_two * scale)
+    grad_one, grad_two = all_sum(part_one, part_two, scale)
+    return (d_volume, grad_one, grad_two)
 
 
 def solution(mesh):

time: 407 us -> 169 us (0.42)
  waiting for transfers between devices: 277 us -> 12.2 us
  Pallas kernels: 0 us -> 47.1 us
  between operations: 15.4 us -> 1.99 us
  other arithmetic: 18.7 us -> 7.31 us
  matrix products: 17.8 us -> 23.3 us
    psum x1 -> x0, waiting for transfers between devices: 263 us -> none  [body(): summed_one, summed_two = lax.psum((part_one, part_two), ('ta', 'ha', 'wa'))]
    pallas_call x0 -> x1, Pallas kernels: none -> 47.1 us  [all_sum(): pl.pallas_call(reduce_kernel, out_shape=(shape, shape), in_specs=[pl.Bloc...]
    reshape x18, local copies, waits for them, and re-layouts: 22.8 us -> 13.3 us  [window_rows(): return jnp.concatenate(pieces, axis=-1).reshape(-1, 3 * chans)]
    dot_general x18, matrix products: 4.65 us -> 12.9 us  [kernel_local(): lax.dot_general(rows, right, (((0,), (0,)), ((), ())), preferred_element_...]
    concatenate x16, other arithmetic: 10.8 us -> 2.69 us  [window_rows(): return jnp.concatenate(pieces, axis=-1).reshape(-1, 3 * chans)]
    unnamed x130 -> x154, local copies, waits for them, and re-layouts: 6.02 us -> 10.6 us
    mul x2, other arithmetic: 4.5 us -> 0.32 us  [from_slots(): tiles = jnp.swapaxes(tiles, 0, 1).astype(F32) * scale]
  transfers between devices with their start and end apart: 13 -> 12, of which waited for: 5 -> 5; matrix products, arithmetic and copies ran while one was open for 5% -> 8% of each run, Pallas kernels for 0% -> 28%
where the time goes in v1:
time: 169 us; the launch traced here: 168 us
  Pallas kernels  47.1 us (28%)
  local copies, waits for them, and re-layouts  41.5 us (25%)
  starting transfers between devices  34.2 us (20%)
  matrix products  23.3 us (14%)
  waiting for transfers between devices  12.2 us (7%)
  other arithmetic  7.31 us (4%)
  between operations  1.99 us (1%)
    pallas_call x1, Pallas kernels, all_sum(): pl.pallas_call(reduce_kernel, out_shape=(shape, shape), in_specs=[pl.Bloc...  47.1 us
    ppermute x6, starting transfers between devices, padded_2(): lax.ppermute(tail, axis, [(i, (i + 1) % count) for i in range(ends)])  25.1 us
    reshape x18, local copies, waits for them, and re-layouts, window_rows(): return jnp.concatenate(pieces, axis=-1).reshape(-1, 3 * chans)  13.3 us
    dot_general x18, matrix products, kernel_local(): lax.dot_general(rows, right, (((0,), (0,)), ((), ())), preferred_element_...  12.9 us
    ppermute x6, waiting for transfers between devices, padded_2(): lax.ppermute(head, axis, [((i + 1) % count, i) for i in range(ends)])  12.2 us
    unnamed x154, local copies, waits for them, and re-layouts  10.6 us
    dot_general x27, matrix products, conv_local(): jnp.dot(rows, kernel[offset_t, offset_h].reshape(3 * chans, chans), prefe...  10.3 us
    ppermute x6, starting transfers between devices, padded_2(): lax.ppermute(head, axis, [((i + 1) % count, i) for i in range(ends)])  9.14 us
  transfers between devices with their start and end apart: 12, of which 5 were waited for; matrix products, arithmetic and copies ran while one was open for 8% of the time, Pallas kernels for 28%

profile of v1, /device:TPU:1, one launch (start us, length us, event | category | flops | bytes accessed | tf_op | source)
XLA Modules:
  0.0 167.6 jit_solution(8974877234312038216)
XLA Ops:
  1.7 3.9 %collective-permute-start = (bf16[2,1,32,16,128]{4,3,2,1,0:T(8,128)(2,1)S(1)}, bf16[2,1,32,16,128]{4,3,2,1,0:T(8,128)(2,1)S(1)}, u32[]{:S(2)}, u32[]{:S(2)}) collective-permute-start(bf16[2,1,32,16,128]{4,3,2,1,0:T(8,128)(2,1)S(1)} %pad_maximum_fusion.40), channel_id=1, source_target_pairs={{0,32},{32,64},{64,96},{96,128},{128,160},{160,192},{192,224},{1,3... | collective-permute-start | bytes 786440 | tf_op jit(solution)/shard_map/ppermute | solution.py:23
  7.0 2.2 %fusion.66 = (bf16[1,1,3,128,128]{4,3,2,1,0:T(8,128)(2,1)}, bf16[1,1,3,128,128]{4,3,2,1,0:T(8,128)(2,1)}, bf16[1,1,3,128,128]{4,3,2,1,0:T(8,128)(2,1)}, bf16[1,1...) fusion(bf16[3,3,3,128,128]{4,3,2,1,0:T(8,128)(2,1)} %param.6), kind=kLoop, calls=%fused_computation.183 | loop fusion | bytes 1769472 | tf_op jit(solution)/shard_map/slice | solution.py:59
  9.2 1.4 copy.25
  11.7 1.4 copy.26
  14.5 3.2 %collective-permute-start.2 = (bf16[2,3,1,16,128]{4,3,2,1,0:T(8,128)(2,1)S(1)}, bf16[2,3,1,16,128]{4,3,2,1,0:T(8,128)(2,1)S(1)}, u32[]{:S(2)}, u32[]{:S(2)}) collective-permute-start(bf16[2,3,1,16,128]{4,3,2,1,0:T(8,128)(2,1)S(1)} %get-tuple-element.38), channel_id=1, source_target_pairs={{0,8},{8,16},{16,24},{1,9},{9,17},{17,25},{2,10},{10,18},{18,26},{... | collective-permute-start | bytes 73736 | tf_op jit(solution)/shard_map/ppermute | solution.py:23
  19.1 3.2 %collective-permute-done.3 = bf16[2,3,1,16,128]{4,3,2,1,0:T(8,128)(2,1)S(1)} collective-permute-done((bf16[2,3,1,16,128]{4,3,2,1,0:T(8,128)(2,1)S(1)}, bf16[2,3,1,16,128]{4,3,2,1,0:T(8,128)(2,1)S(1)}, u32[]{:S(2)}, u32[]{:S(2)}) %collective-permute-start.3) | collective-permute-done | bytes 24608 | tf_op jit(solution)/shard_map/ppermute | solution.py:25
  22.4 8.0 %collective-permute-start.4 = (bf16[2,3,34,1,128]{4,3,2,1,0:T(2,128)(2,1)S(1)}, bf16[2,3,34,1,128]{4,3,2,1,0:T(2,128)(2,1)S(1)}, u32[]{:S(2)}, u32[]{:S(2)}) collective-permute-start(bf16[2,3,34,1,128]{4,3,2,1,0:T(2,128)(2,1)S(1)} %get-tuple-element.36), channel_id=1, source_target_pairs={{0,1},{1,2},{2,3},{3,4},{4,5},{5,6},{6,7},{8,9},{9,10},{10,11},{11... | collective-permute-start | bytes 156680 | tf_op jit(solution)/shard_map/ppermute | solution.py:23
  30.5 1.9 %collective-permute-start.5 = (bf16[2,3,34,1,128]{4,3,2,1,0:T(2,128)(2,1)S(1)}, bf16[2,3,34,1,128]{4,3,2,1,0:T(2,128)(2,1)S(1)}, u32[]{:S(2)}, u32[]{:S(2)}) collective-permute-start(bf16[2,3,34,1,128]{4,3,2,1,0:T(2,128)(2,1)S(1)} %get-tuple-element.37), channel_id=1, source_target_pairs={{1,0},{2,1},{3,2},{4,3},{5,4},{6,5},{7,6},{9,8},{10,9},{11,10},{12... | collective-permute-start | bytes 156680 | tf_op jit(solution)/shard_map/ppermute | solution.py:25
  33.6 3.8 %collective-permute-done.5 = bf16[2,3,34,1,128]{4,3,2,1,0:T(2,128)(2,1)S(1)} collective-permute-done((bf16[2,3,34,1,128]{4,3,2,1,0:T(2,128)(2,1)S(1)}, bf16[2,3,34,1,128]{4,3,2,1,0:T(2,128)(2,1)S(1)}, u32[]{:S(2)}, u32[]{:S(2)}) %collective-permute-start.5) | collective-permute-done | bytes 52256 | tf_op jit(solution)/shard_map/ppermute | solution.py:25
  40.5 1.5 fusion.69
  73.8 2.1 %fusion.9 = bf16[9,3,128,128]{3,2,1,0:T(8,128)(2,1)} fusion(bf16[3,128,512]{2,1,0:T(8,128)(2,1)} %bitcast.393, bf16[512,128]{1,0:T(8,128)(2,1)S(1)} %get-tuple-element.124), kind=kOutput, calls=%fused_computation.46 | convolution fusion | flops 50331648 | bytes 720896 | tf_op jit(solution)/shard_map/dot_general | solution.py:72
  75.9 1.9 %fusion.8 = bf16[9,3,128,128]{3,2,1,0:T(8,128)(2,1)} fusion(bf16[9,3,128,128]{3,2,1,0:T(8,128)(2,1)} %fusion.9, bf16[3,128,512]{2,1,0:T(8,128)(2,1)} %bitcast.394, bf16[512,128]{1,0:T(8,128)(2,1)S(1)} %get-tuple-element.124), kind=kOutput, calls=%fused_computation.44 | convolution fusion | flops 50331648 | bytes 720896 | tf_op jit(solution)/shard_map/dot_general | solution.py:72
  84.1 2.0 %copy.46 = bf16[3,3,3,128,128]{3,4,2,1,0:T(8,128)(2,1)S(1)} copy(bf16[3,3,3,128,128]{4,3,2,1,0:T(8,128)(2,1)} %bitcast.122) | data formatting | bytes 1769472 | tf_op jit(solution)/shard_map/reshape | solution.py:76
  87.5 3.2 %collective-permute-start.6 = (bf16[1,32,16,128]{3,2,1,0:T(8,128)(2,1)S(1)}, bf16[1,32,16,128]{3,2,1,0:T(8,128)(2,1)S(1)}, u32[]{:S(2)}, u32[]{:S(2)}) collective-permute-start(bf16[1,32,16,128]{3,2,1,0:T(8,128)(2,1)S(1)} %multiply_convert_fusion.2), channel_id=1, source_target_pairs={{0,32},{32,64},{64,96},{96,128},{128,160},{160,192},{192,224},{1,3... | collective-permute-start | bytes 393224 | tf_op jit(solution)/shard_map/ppermute | solution.py:23
  92.0 1.6 maximum_maximum_fusion.1
  93.7 47.1 %shard_map.67 = (bf16[8,32,16,128]{3,2,1,0:T(8,128)(2,1)}, bf16[8,32,16,128]{3,2,1,0:T(8,128)(2,1)}) custom-call(bf16[8,32,16,128]{3,2,1,0:T(8,128)(2,1)} %get-tuple-element.127.one, bf16[8,32,16,128]{3,2,1,0:T(8,128)(2,1)} %get-tuple-element.126.two), custom_call_target="tpu_custom_call" | custom-call | tf_op jit(solution)/shard_map/pallas_call | solution.py:341
  142.9 2.4 %collective-permute-start.8 = (bf16[3,1,16,128]{3,2,1,0:T(8,128)(2,1)S(1)}, bf16[3,1,16,128]{3,2,1,0:T(8,128)(2,1)S(1)}, u32[]{:S(2)}, u32[]{:S(2)}) collective-permute-start(bf16[3,1,16,128]{3,2,1,0:T(8,128)(2,1)S(1)} %get-tuple-element.123), channel_id=1, source_target_pairs={{0,8},{8,16},{16,24},{1,9},{9,17},{17,25},{2,10},{10,18},{18,26},{... | collective-permute-start | bytes 36872 | tf_op jit(solution)/shard_map/ppermute | solution.py:23
  145.3 1.4 collective-permute-start.9
  147.0 2.9 %collective-permute-done.9 = bf16[3,1,16,128]{3,2,1,0:T(8,128)(2,1)S(1)} collective-permute-done((bf16[3,1,16,128]{3,2,1,0:T(8,128)(2,1)S(1)}, bf16[3,1,16,128]{3,2,1,0:T(8,128)(2,1)S(1)}, u32[]{:S(2)}, u32[]{:S(2)}) %collective-permute-start.9) | collective-permute-done | bytes 12320 | tf_op jit(solution)/shard_map/ppermute | solution.py:25
  149.9 4.4 %collective-permute-start.10 = (bf16[3,34,1,128]{3,2,1,0:T(2,128)(2,1)S(1)}, bf16[3,34,1,128]{3,2,1,0:T(2,128)(2,1)S(1)}, u32[]{:S(2)}, u32[]{:S(2)}) collective-permute-start(bf16[3,34,1,128]{3,2,1,0:T(2,128)(2,1)S(1)} %get-tuple-element.114), channel_id=1, source_target_pairs={{0,1},{1,2},{2,3},{3,4},{4,5},{5,6},{6,7},{8,9},{9,10},{10,11},{11... | collective-permute-start | bytes 78344 | tf_op jit(solution)/shard_map/ppermute | solution.py:23
  154.3 1.9 %collective-permute-start.11 = (bf16[3,34,1,128]{3,2,1,0:T(2,128)(2,1)S(1)}, bf16[3,34,1,128]{3,2,1,0:T(2,128)(2,1)S(1)}, u32[]{:S(2)}, u32[]{:S(2)}) collective-permute-start(bf16[3,34,1,128]{3,2,1,0:T(2,128)(2,1)S(1)} %get-tuple-element.115), channel_id=1, source_target_pairs={{1,0},{2,1},{3,2},{4,3},{5,4},{6,5},{7,6},{9,8},{10,9},{11,10},{12... | collective-permute-start | bytes 78344 | tf_op jit(solution)/shard_map/ppermute | solution.py:25
  156.4 1.4 copy.49
  157.8 1.4 copy.48
  159.2 1.9 %collective-permute-done.11 = bf16[3,34,1,128]{3,2,1,0:T(2,128)(2,1)S(1)} collective-permute-done((bf16[3,34,1,128]{3,2,1,0:T(2,128)(2,1)S(1)}, bf16[3,34,1,128]{3,2,1,0:T(2,128)(2,1)S(1)}, u32[]{:S(2)}, u32[]{:S(2)}) %collective-permute-start.11) | collective-permute-done | bytes 26144 | tf_op jit(solution)/shard_map/ppermute | solution.py:25
  (274 shorter events, 59.5 us)
Async XLA Ops:
  0.6 8.5 %copy-start.22 = (bf16[3,3,3,128,128]{4,3,2,1,0:T(8,128)(2,1)S(1)}, bf16[3,3,3,128,128]{4,3,2,1,0:T(8,128)(2,1)}, u32[]{:S(2)}) copy-start(bf16[3,3,3,128,128]{4,3,2,1,0:T(8,128)(2,1)} %param.7) | copy-start | bytes 2654212
  1.7 12.4 %collective-permute-start = (bf16[2,1,32,16,128]{4,3,2,1,0:T(8,128)(2,1)S(1)}, bf16[2,1,32,16,128]{4,3,2,1,0:T(8,128)(2,1)S(1)}, u32[]{:S(2)}, u32[]{:S(2)}) collective-permute-start(bf16[2,1,32,16,128]{4,3,2,1,0:T(8,128)(2,1)S(1)} %pad_maximum_fusion.40), channel_id=1, source_target_pairs={{0,32},{32,64},{64,96},{96,128},{128,160},{160,192},{192,224},{1,3... | collective-permute-start | bytes 786440 | tf_op jit(solution)/shard_map/ppermute | solution.py:23
  5.7 8.8 %collective-permute-start.1 = (bf16[2,1,32,16,128]{4,3,2,1,0:T(8,128)(2,1)S(1)}, bf16[2,1,32,16,128]{4,3,2,1,0:T(8,128)(2,1)S(1)}, u32[]{:S(2)}, u32[]{:S(2)}) collective-permute-start(bf16[2,1,32,16,128]{4,3,2,1,0:T(8,128)(2,1)S(1)} %pad_maximum_fusion.40), channel_id=1, source_target_pairs={{32,0},{64,32},{96,64},{128,96},{160,128},{192,160},{224,192},{33,... | collective-permute-start | bytes 786440 | tf_op jit(solution)/shard_map/ppermute | solution.py:25
  14.5 4.6 %collective-permute-start.2 = (bf16[2,3,1,16,128]{4,3,2,1,0:T(8,128)(2,1)S(1)}, bf16[2,3,1,16,128]{4,3,2,1,0:T(8,128)(2,1)S(1)}, u32[]{:S(2)}, u32[]{:S(2)}) collective-permute-start(bf16[2,3,1,16,128]{4,3,2,1,0:T(8,128)(2,1)S(1)} %get-tuple-element.38), channel_id=1, source_target_pairs={{0,8},{8,16},{16,24},{1,9},{9,17},{17,25},{2,10},{10,18},{18,26},{... | collective-permute-start | bytes 73736 | tf_op jit(solution)/shard_map/ppermute | solution.py:23
  17.7 4.6 %collective-permute-start.3 = (bf16[2,3,1,16,128]{4,3,2,1,0:T(8,128)(2,1)S(1)}, bf16[2,3,1,16,128]{4,3,2,1,0:T(8,128)(2,1)S(1)}, u32[]{:S(2)}, u32[]{:S(2)}) collective-permute-start(bf16[2,3,1,16,128]{4,3,2,1,0:T(8,128)(2,1)S(1)} %get-tuple-element.39), channel_id=1, source_target_pairs={{8,0},{16,8},{24,16},{9,1},{17,9},{25,17},{10,2},{18,10},{26,18},{... | collective-permute-start | bytes 73736 | tf_op jit(solution)/shard_map/ppermute | solution.py:25
  22.4 11.1 %collective-permute-start.4 = (bf16[2,3,34,1,128]{4,3,2,1,0:T(2,128)(2,1)S(1)}, bf16[2,3,34,1,128]{4,3,2,1,0:T(2,128)(2,1)S(1)}, u32[]{:S(2)}, u32[]{:S(2)}) collective-permute-start(bf16[2,3,34,1,128]{4,3,2,1,0:T(2,128)(2,1)S(1)} %get-tuple-element.36), channel_id=1, source_target_pairs={{0,1},{1,2},{2,3},{3,4},{4,5},{5,6},{6,7},{8,9},{9,10},{10,11},{11... | collective-permute-start | bytes 156680 | tf_op jit(solution)/shard_map/ppermute | solution.py:23
  30.5 6.9 %collective-permute-start.5 = (bf16[2,3,34,1,128]{4,3,2,1,0:T(2,128)(2,1)S(1)}, bf16[2,3,34,1,128]{4,3,2,1,0:T(2,128)(2,1)S(1)}, u32[]{:S(2)}, u32[]{:S(2)}) collective-permute-start(bf16[2,3,34,1,128]{4,3,2,1,0:T(2,128)(2,1)S(1)} %get-tuple-element.37), channel_id=1, source_target_pairs={{1,0},{2,1},{3,2},{4,3},{5,4},{6,5},{7,6},{9,8},{10,9},{11,10},{12... | collective-permute-start | bytes 156680 | tf_op jit(solution)/shard_map/ppermute | solution.py:25
  50.7 3.1 %copy-start.16 = (bf16[1,32,16,384]{3,2,1,0:T(8,128)(2,1)}, bf16[1,32,16,384]{3,2,1,0:T(8,128)(2,1)S(1)}, u32[]{:S(2)}) copy-start(bf16[1,32,16,384]{3,2,1,0:T(8,128)(2,1)S(1)} %get-tuple-element.148) | copy-start | bytes 1179652
  52.6 2.4 %copy-start.72 = (bf16[1,1,3,128,128]{4,3,2,1,0:T(8,128)(2,1)S(1)}, bf16[1,1,3,128,128]{4,3,2,1,0:T(8,128)(2,1)}, u32[]{:S(2)}) copy-start(bf16[1,1,3,128,128]{4,3,2,1,0:T(8,128)(2,1)} %get-tuple-element.32) | copy-start | bytes 294916
  53.8 1.5 copy-start.71
  61.7 2.2 %copy-start.1 = (bf16[1,32,16,384]{3,2,1,0:T(8,128)(2,1)}, bf16[1,32,16,384]{3,2,1,0:T(8,128)(2,1)S(1)}, u32[]{:S(2)}) copy-start(bf16[1,32,16,384]{3,2,1,0:T(8,128)(2,1)S(1)} %get-tuple-element.141) | copy-start | bytes 1179652
  62.8 1.4 copy-start.20
  62.9 1.6 copy-start.9
  73.5 4.2 %copy-start.19 = (bf16[512,384]{0,1:T(8,128)(2,1)S(1)}, bf16[512,384]{0,1:T(8,128)(2,1)}, u32[]{:S(2)}) copy-start(bf16[512,384]{0,1:T(8,128)(2,1)} %copy.39) | copy-start | bytes 1179652
  73.8 4.9 %copy-start.18 = (bf16[512,384]{0,1:T(8,128)(2,1)S(1)}, bf16[512,384]{0,1:T(8,128)(2,1)}, u32[]{:S(2)}) copy-start(bf16[512,384]{0,1:T(8,128)(2,1)} %copy.40) | copy-start | bytes 1179652
  86.4 5.6 %copy-start.5 = (bf16[8,14,16,128]{3,2,1,0:T(8,128)(2,1)S(1)}, bf16[8,14,16,128]{3,2,1,0:T(8,128)(2,1)}, u32[]{:S(2)}) copy-start(bf16[8,14,16,128]{3,2,1,0:T(8,128)(2,1)} %slice.662) | copy-start | bytes 1376260
  86.4 5.6 %copy-start.6 = (bf16[8,13,16,128]{3,2,1,0:T(8,128)(2,1)S(1)}, bf16[8,13,16,128]{3,2,1,0:T(8,128)(2,1)}, u32[]{:S(2)}) copy-start(bf16[8,13,16,128]{3,2,1,0:T(8,128)(2,1)} %slice.663) | copy-start | bytes 1277956
  87.5 55.3 %collective-permute-start.6 = (bf16[1,32,16,128]{3,2,1,0:T(8,128)(2,1)S(1)}, bf16[1,32,16,128]{3,2,1,0:T(8,128)(2,1)S(1)}, u32[]{:S(2)}, u32[]{:S(2)}) collective-permute-start(bf16[1,32,16,128]{3,2,1,0:T(8,128)(2,1)S(1)} %multiply_convert_fusion.2), channel_id=1, source_target_pairs={{0,32},{32,64},{64,96},{96,128},{128,160},{160,192},{192,224},{1,3... | collective-permute-start | bytes 393224 | tf_op jit(solution)/shard_map/ppermute | solution.py:23
  90.7 52.1 %collective-permute-start.7 = (bf16[1,32,16,128]{3,2,1,0:T(8,128)(2,1)S(1)}, bf16[1,32,16,128]{3,2,1,0:T(8,128)(2,1)S(1)}, u32[]{:S(2)}, u32[]{:S(2)}) collective-permute-start(bf16[1,32,16,128]{3,2,1,0:T(8,128)(2,1)S(1)} %multiply_convert_fusion.2), channel_id=1, source_target_pairs={{32,0},{64,32},{96,64},{128,96},{160,128},{192,160},{224,192},{33,... | collective-permute-start | bytes 393224 | tf_op jit(solution)/shard_map/ppermute | solution.py:25
  142.9 4.1 %collective-permute-start.8 = (bf16[3,1,16,128]{3,2,1,0:T(8,128)(2,1)S(1)}, bf16[3,1,16,128]{3,2,1,0:T(8,128)(2,1)S(1)}, u32[]{:S(2)}, u32[]{:S(2)}) collective-permute-start(bf16[3,1,16,128]{3,2,1,0:T(8,128)(2,1)S(1)} %get-tuple-element.123), channel_id=1, source_target_pairs={{0,8},{8,16},{16,24},{1,9},{9,17},{17,25},{2,10},{10,18},{18,26},{... | collective-permute-start | bytes 36872 | tf_op jit(solution)/shard_map/ppermute | solution.py:23
  145.3 1.6 copy-start.23
  145.3 4.6 %collective-permute-start.9 = (bf16[3,1,16,128]{3,2,1,0:T(8,128)(2,1)S(1)}, bf16[3,1,16,128]{3,2,1,0:T(8,128)(2,1)S(1)}, u32[]{:S(2)}, u32[]{:S(2)}) collective-permute-start(bf16[3,1,16,128]{3,2,1,0:T(8,128)(2,1)S(1)} %get-tuple-element.122), channel_id=1, source_target_pairs={{8,0},{16,8},{24,16},{9,1},{17,9},{25,17},{10,2},{18,10},{26,18},{... | collective-permute-start | bytes 36872 | tf_op jit(solution)/shard_map/ppermute | solution.py:25
  149.9 9.3 %collective-permute-start.10 = (bf16[3,34,1,128]{3,2,1,0:T(2,128)(2,1)S(1)}, bf16[3,34,1,128]{3,2,1,0:T(2,128)(2,1)S(1)}, u32[]{:S(2)}, u32[]{:S(2)}) collective-permute-start(bf16[3,34,1,128]{3,2,1,0:T(2,128)(2,1)S(1)} %get-tuple-element.114), channel_id=1, source_target_pairs={{0,1},{1,2},{2,3},{3,4},{4,5},{5,6},{6,7},{8,9},{9,10},{10,11},{11... | collective-permute-start | bytes 78344 | tf_op jit(solution)/shard_map/ppermute | solution.py:23
  154.3 6.8 %collective-permute-start.11 = (bf16[3,34,1,128]{3,2,1,0:T(2,128)(2,1)S(1)}, bf16[3,34,1,128]{3,2,1,0:T(2,128)(2,1)S(1)}, u32[]{:S(2)}, u32[]{:S(2)}) collective-permute-start(bf16[3,34,1,128]{3,2,1,0:T(2,128)(2,1)S(1)} %get-tuple-element.115), channel_id=1, source_target_pairs={{1,0},{2,1},{3,2},{4,3},{5,4},{6,5},{7,6},{9,8},{10,9},{11,10},{12... | collective-permute-start | bytes 78344 | tf_op jit(solution)/shard_map/ppermute | solution.py:25
  (64 other events, 68.0 us)

commit v2 on v1

--- a/solution.py
+++ b/solution.py
@@ -1,5 +1,3 @@
-import functools
-
 import jax
 import jax.numpy as jnp
 from jax import lax
@@ -10,70 +8,6 @@
 MESH = pl.DeviceIdType.MESH
 F32 = jnp.float32
 BF16 = jnp.bfloat16
-
-
-def padded_2(cells, sides, width):
-    for axis, dim in sides:
-        count = lax.axis_size(axis)
-        ends = count - 1
-        head = lax.slice_in_dim(cells, 0, width, axis=dim)
-        tail = lax.slice_in_dim(cells, cells.shape[dim] - width, cells.shape[dim], axis=dim)
-        cells = jnp.concatenate(
-            [
-                lax.ppermute(tail, axis, [(i, (i + 1) % count) for i in range(ends)]),
-                cells,
-                lax.ppermute(head, axis, [((i + 1) % count, i) for i in range(ends)]),
-            ],
-            axis=dim,
-        )
-    return cells
-
-
-def flip_swap(kernel):
-    return jnp.swapaxes(kernel[::-1, ::-1, ::-1], 3, 4)
-
-
-def window_rows(padded, offset_t, offset_h):
-    frames = padded.shape[0] - 2
-    height = padded.shape[1] - 2
-    width = padded.shape[2] - 2
-    chans = padded.shape[3]
-    pieces = [
-        padded[offset_t : offset_t + frames, offset_h : offset_h + height, shift : shift + width]
-        for shift in range(3)
-    ]
-    return jnp.concatenate(pieces, axis=-1).reshape(-1, 3 * chans)
-
-
-def conv_local(padded, kernel):
-    frames = padded.shape[0] - 2
-    height = padded.shape[1] - 2
-    width = padded.shape[2] - 2
-    chans = padded.shape[3]
-    total = jnp.zeros((frames * height * width, chans), jnp.float32)
-    for offset_t in range(3):
-        for offset_h in range(3):
-            rows = window_rows(padded, offset_t, offset_h)
-            total = total + jnp.dot(
-                rows,
-                kernel[offset_t, offset_h].reshape(3 * chans, chans),
-                preferred_element_type=jnp.float32,
-            )
-    return total.reshape(frames, height, width, chans)
-
-
-def kernel_local(padded, other):
-    chans = padded.shape[3]
-    right = other.reshape(-1, chans)
-    blocks = []
-    for offset_t in range(3):
-        for offset_h in range(3):
-            rows = window_rows(padded, offset_t, offset_h)
-            product = lax.dot_general(
-                rows, right, (((0,), (0,)), ((), ())), preferred_element_type=jnp.float32
-            )
-            blocks.append(product.reshape(3, chans, chans))
-    return jnp.stack(blocks).reshape(3, 3, 3, chans, chans)
 
 
 class Place:
@@ -97,6 +31,9 @@
     def peer_z(self, off):
         to = lax.rem(self.z + off, 8)
         return to, (lax.rem(to, 2) * 4 + self.x, self.ha, (to // 2) * 2 + self.core)
+
+    def near(self, dta, dha, dwa):
+        return (lax.rem(self.ta + dta + 8, 8), lax.rem(self.ha + dha + 4, 4), lax.rem(self.wa + dwa + 8, 8))
 
     def twin(self):
         return (self.ta, self.ha, self.wa + 1 - 2 * self.core)
@@ -272,13 +209,6 @@
 ]
 
 
-def enter(place, others):
-    barrier = pltpu.get_barrier_semaphore()
-    for device in others:
-        pl.semaphore_signal(barrier, inc=1, device_id=device, device_id_type=MESH)
-    pl.semaphore_wait(barrier, len(others))
-
-
 def reduce_peers(place):
     peers = [place.twin()]
     peers += [place.peer_x(off)[1] for off in range(1, 4)]
@@ -287,47 +217,321 @@
     return peers
 
 
-def reduce_kernel(one, two, full_one, full_two, *scratch):
+class Field:
+    def __init__(self, place, raw, wide, cols, ends, cols_out, ends_out, win, sends, recvs):
+        self.at = place
+        self.raw, self.wide = raw, wide
+        self.cols, self.ends, self.cols_out, self.ends_out = cols, ends, cols_out, ends_out
+        self.win, self.sends, self.recvs = win, sends, recvs
+
+    def stage(self):
+        own = self.raw[1, pl.ds(1, 32)].astype(F32)
+        self.wide[...] = own.reshape(512, 128)
+        self.cols_out[0] = self.wide[pl.ds(0, 32, stride=16), :].astype(BF16)
+        self.cols_out[1] = self.wide[pl.ds(15, 32, stride=16), :].astype(BF16)
+        self.ends_out[0] = self.wide[pl.ds(0, 1), :]
+        self.ends_out[1] = self.wide[pl.ds(496, 1), :]
+        self.ends_out[2] = self.wide[pl.ds(15, 1), :]
+        self.ends_out[3] = self.wide[pl.ds(511, 1), :]
+
+    def go(self, kind, src, dst, device):
+        send(src, dst, self.sends.at[kind], self.recvs.at[kind], device)
+
+    def frame_send(self):
+        near = self.at.near
+        self.go(0, self.raw.at[1, 1], self.raw.at[1, 33], near(0, -1, 0))
+        self.go(0, self.raw.at[1, 32], self.raw.at[1, 0], near(0, 1, 0))
+        self.go(1, self.cols_out.at[0], self.cols.at[1, 1], near(0, 0, -1))
+        self.go(1, self.cols_out.at[1], self.cols.at[1, 0], near(0, 0, 1))
+        self.go(2, self.ends_out.at[0], self.ends.at[1, 3], near(0, -1, -1))
+        self.go(2, self.ends_out.at[1], self.ends.at[1, 2], near(0, 1, -1))
+        self.go(2, self.ends_out.at[2], self.ends.at[1, 1], near(0, -1, 1))
+        self.go(2, self.ends_out.at[3], self.ends.at[1, 0], near(0, 1, 1))
+
+    def bulk_send(self):
+        near = self.at.near
+        own = self.raw.at[1, pl.ds(1, 32)]
+        self.go(3, own, self.raw.at[0, pl.ds(1, 32)], near(1, 0, 0))
+        self.go(3, own, self.raw.at[2, pl.ds(1, 32)], near(-1, 0, 0))
+
+    def frame_wait(self):
+        wait_bytes(self.raw.at[1, pl.ds(0, 2)], self.recvs.at[0])
+        wait_bytes(self.cols.at[1], self.recvs.at[1])
+        wait_bytes(self.ends.at[1], self.recvs.at[2])
+
+    def rim_send(self):
+        for frame, step in ((0, 1), (2, -1)):
+            device = self.at.near(step, 0, 0)
+            self.go(4, self.raw.at[1, 0], self.raw.at[frame, 0], device)
+            self.go(4, self.raw.at[1, 33], self.raw.at[frame, 33], device)
+            self.go(5, self.cols.at[1], self.cols.at[frame], device)
+            self.go(6, self.ends.at[1], self.ends.at[frame], device)
+
+    def times_wait(self):
+        wait_bytes(self.raw.at[pl.ds(0, 2), pl.ds(0, 32)], self.recvs.at[3])
+        wait_bytes(self.raw.at[0, pl.ds(0, 4)], self.recvs.at[4])
+        wait_bytes(self.cols.at[pl.ds(0, 2)], self.recvs.at[5])
+        wait_bytes(self.ends.at[pl.ds(0, 2)], self.recvs.at[6])
+
+    def drain(self):
+        wait_bytes(self.raw.at[1, pl.ds(0, 2)], self.sends.at[0])
+        wait_bytes(self.cols.at[1], self.sends.at[1])
+        wait_bytes(self.ends.at[1], self.sends.at[2])
+        wait_bytes(self.raw.at[pl.ds(0, 2), pl.ds(0, 32)], self.sends.at[3])
+        wait_bytes(self.raw.at[0, pl.ds(0, 4)], self.sends.at[4])
+        wait_bytes(self.cols.at[pl.ds(0, 2)], self.sends.at[5])
+        wait_bytes(self.ends.at[pl.ds(0, 2)], self.sends.at[6])
+
+    def windows(self, frame):
+        spot = lax.broadcasted_iota(jnp.int32, (16, 128), 0)
+        at_left, at_right = self.at.wa == 0, self.at.wa == 7
+
+        def line(row, left, right):
+            mid = self.raw[frame, row]
+            wide = mid.astype(F32)
+            left = jnp.where(at_left, 0.0, left)
+            right = jnp.where(at_right, 0.0, right)
+            before = jnp.where(spot == 0, left, pltpu.roll(wide, 1, 0))
+            after = jnp.where(spot == 15, right, pltpu.roll(wide, 15, 0))
+            self.win[frame, row, :, pl.ds(0, 128)] = before.astype(BF16)
+            self.win[frame, row, :, pl.ds(128, 128)] = mid
+            self.win[frame, row, :, pl.ds(256, 128)] = after.astype(BF16)
+
+        def group(g, _):
+            start = pl.multiple_of(16 * g, 16)
+            left = self.cols[frame, 0, pl.ds(start, 16), :].astype(F32)
+            right = self.cols[frame, 1, pl.ds(start, 16), :].astype(F32)
+            for r in range(16):
+                line(16 * g + r + 1, left[r : r + 1], right[r : r + 1])
+            return 0
+
+        lax.fori_loop(0, 2, group, 0)
+        line(0, self.ends[frame, 0], self.ends[frame, 2])
+        line(33, self.ends[frame, 1], self.ends[frame, 3])
+        blank = jnp.zeros((16, 384), BF16)
+
+        @pl.when(self.at.ha == 0)
+        def _():
+            self.win[frame, 0] = blank
+
+        @pl.when(self.at.ha == 3)
+        def _():
+            self.win[frame, 33] = blank
+
+        if frame != 1:
+
+            @pl.when(self.at.ta == (0 if frame == 0 else 7))
+            def _():
+                self.win[frame] = jnp.zeros((34, 16, 384), BF16)
+
+    def taps(self, weights, frame):
+        rows = [weights[pl.ds(9 * frame + 3 * kh, 3)].reshape(384, 128) for kh in range(3)]
+        return jnp.concatenate(rows, axis=1)
+
+    def middle(self, weights, out):
+        lhs = self.win[1].reshape(544, 384)
+        out[...] = jnp.dot(lhs, self.taps(weights, 1), preferred_element_type=F32).reshape(34, 16, 384)
+
+    def outer(self, weights, out):
+        lhs = jnp.concatenate([self.win[0].reshape(544, 384), self.win[2].reshape(544, 384)], axis=1)
+        rhs = jnp.concatenate([self.taps(weights, 0), self.taps(weights, 2)], axis=0)
+        out[...] = out[...] + jnp.dot(lhs, rhs, preferred_element_type=F32).reshape(34, 16, 384)
+
+
+FIELD_SCRATCH = [
+    pltpu.VMEM((3, 34, 16, 128), BF16),
+    pltpu.VMEM((512, 128), F32),
+    pltpu.VMEM((3, 2, 32, 128), BF16),
+    pltpu.VMEM((3, 4, 1, 128), F32),
+    pltpu.VMEM((2, 32, 128), BF16),
+    pltpu.VMEM((4, 1, 128), F32),
+    pltpu.VMEM((3, 34, 16, 384), BF16),
+    pltpu.SemaphoreType.DMA((7,)),
+    pltpu.SemaphoreType.DMA((7,)),
+]
+
+
+def shifted(out, row):
+    return (
+        out[pl.ds(row, 4), :, pl.ds(0, 128)]
+        + out[pl.ds(row + 1, 4), :, pl.ds(128, 128)]
+        + out[pl.ds(row + 2, 4), :, pl.ds(256, 128)]
+    )
+
+
+def slot_of(tap):
+    return tap if tap < 14 else tap + 2
+
+
+def transposed(weights, out):
+    def step(n, _):
+        out[n] = weights[26 - n].T
+        return 0
+
+    lax.fori_loop(0, 27, step, 0)
+
+
+def block_kernel(vol_hbm, cot_hbm, one_hbm, two_hbm, d_vol, full_one, full_two, *scratch):
     place = Place()
-    enter(place, reduce_peers(place))
-    size = len(REDUCE_SCRATCH)
-    grads = [
-        Reduce(place, two, full_two, *scratch[:size]),
-        Reduce(place, one, full_one, *scratch[size:]),
+    barrier = pltpu.get_barrier_semaphore()
+    others = reduce_peers(place)
+    others += [place.near(s, 0, 0) for s in (1, -1)]
+    others += [place.near(0, 0, s) for s in (1, -1)]
+    others += [place.near(0, a, b) for a in (1, -1) for b in (1, -1)]
+    for device in others:
+        pl.semaphore_signal(barrier, inc=1, device_id=device, device_id_type=MESH)
+
+    f, r = len(FIELD_SCRATCH), len(REDUCE_SCRATCH)
+    vol = Field(place, *scratch[:f])
+    cot = Field(place, *scratch[f : 2 * f])
+    dpre = Field(place, *scratch[2 * f : 3 * f])
+    scratch = scratch[3 * f :]
+    part_one, part_two = scratch[0], scratch[1]
+    red_two = Reduce(place, part_two, full_two, *scratch[2 : 2 + r])
+    red_one = Reduce(place, part_one, full_one, *scratch[2 + r : 2 + 2 * r])
+    scratch = scratch[2 + 2 * r :]
+    one, two, one_t, two_t, out_v, out_c, gate, act, act_t, local = scratch
+
+    loads = [
+        pltpu.make_async_copy(vol_hbm, vol.raw.at[1, pl.ds(1, 32)], local.at[0]),
+        pltpu.make_async_copy(cot_hbm, cot.raw.at[1, pl.ds(1, 32)], local.at[1]),
+        pltpu.make_async_copy(two_hbm, two, local.at[2]),
+        pltpu.make_async_copy(one_hbm, one, local.at[3]),
     ]
-    todo = [(g, s) for g in grads for s in range(2)]
-    for g in grads:
-        g.pair_send()
-    for g, s in todo:
-        g.pair_sum(s)
-        g.first_send(s)
-    for g, s in todo:
-        g.first_sum(s)
-        g.second_send(s)
-    for g, s in todo:
-        g.second_sum(s)
-        g.third_send(s)
-    for g, s in todo:
-        g.third_sum(s)
-        g.third_gather(s)
-    for g, s in todo:
-        g.second_gather(s)
-    for g, s in todo:
-        g.first_gather(s)
-    for g, s in todo:
-        g.pair_gather(s)
-    for g, s in todo:
-        g.finish(s)
-    for g, s in todo:
-        g.drain(s)
-
-
-def to_slots(grad):
-    tiles = grad.reshape(27, 8, 16, 128).astype(BF16)
-    tiles = jnp.swapaxes(tiles, 0, 1)
-    hole = jnp.zeros((8, 2, 16, 128), BF16)
-    last = jnp.zeros((8, 3, 16, 128), BF16)
-    return jnp.concatenate([tiles[:, :14], hole, tiles[:, 14:], last], axis=1)
+    for load in loads:
+        load.start()
+    part_one[:, 29] = jnp.zeros((8, 16, 128), BF16)
+    part_two[:, 29] = jnp.zeros((8, 16, 128), BF16)
+    loads[0].wait()
+    vol.stage()
+    loads[1].wait()
+    cot.stage()
+    pl.semaphore_wait(barrier, len(others))
+
+    vol.bulk_send()
+    vol.frame_send()
+    cot.frame_send()
+    loads[2].wait()
+    transposed(two, two_t)
+    loads[3].wait()
+    vol.frame_wait()
+    vol.rim_send()
+    cot.bulk_send()
+    vol.windows(1)
+    cot.frame_wait()
+    cot.rim_send()
+    cot.windows(1)
+    vol.middle(one, out_v)
+    cot.middle(two_t, out_c)
+    transposed(one, one_t)
+
+    vol.times_wait()
+    vol.windows(0)
+    vol.windows(2)
+    vol.outer(one, out_v)
+
+    def activate(g, _):
+        row = 4 * g
+        pre = shifted(out_v, row)
+        sig = 1.0 / (1.0 + jnp.exp(-pre))
+        act[pl.ds(row, 4)] = (pre * sig).astype(BF16)
+        gate[pl.ds(row, 4)] = sig * (1.0 + pre * (1.0 - sig))
+        return 0
+
+    lax.fori_loop(0, 8, activate, 0)
+    act_t[...] = act[...].reshape(512, 128).T
+
+    cot.times_wait()
+    cot.windows(0)
+    cot.windows(2)
+    for t in range(3):
+        for kh in range(3):
+            rhs = cot.win[t, pl.ds(kh, 32)].reshape(512, 384)
+            got = jnp.dot(act_t[...], rhs, preferred_element_type=F32)
+            for kw in range(3):
+                tap = 26 - (9 * t + 3 * kh + kw)
+                block = got[:, 128 * kw : 128 * kw + 128].reshape(8, 16, 128)
+                part_two[:, slot_of(tap)] = block.astype(BF16)
+    red_two.pair_send()
+
+    cot.outer(two_t, out_c)
+
+    def backward(g, _):
+        row = 4 * g
+        dpre.raw[1, pl.ds(row + 1, 4)] = (shifted(out_c, row) * gate[pl.ds(row, 4)]).astype(BF16)
+        return 0
+
+    lax.fori_loop(0, 8, backward, 0)
+    dpre.stage()
+    dpre.frame_send()
+    act_t[...] = dpre.raw[1, pl.ds(1, 32)].reshape(512, 128).T
+    for s in range(2):
+        red_two.pair_sum(s)
+        red_two.first_send(s)
+    for t in range(3):
+        for kh in range(3):
+            rhs = vol.win[t, pl.ds(kh, 32)].reshape(512, 384)
+            got = jnp.dot(act_t[...], rhs, preferred_element_type=F32)
+            for kw in range(3):
+                tap = 9 * t + 3 * kh + kw
+                block = got[:, 128 * kw : 128 * kw + 128].T.reshape(8, 16, 128)
+                part_one[:, slot_of(tap)] = block.astype(BF16)
+    red_one.pair_send()
+    for s in range(2):
+        red_two.first_sum(s)
+        red_two.second_send(s)
+    for s in range(2):
+        red_one.pair_sum(s)
+        red_one.first_send(s)
+    dpre.frame_wait()
+    dpre.bulk_send()
+    dpre.rim_send()
+    dpre.windows(1)
+    for s in range(2):
+        red_two.second_sum(s)
+        red_two.third_send(s)
+    dpre.middle(one_t, out_v)
+    for s in range(2):
+        red_one.first_sum(s)
+        red_one.second_send(s)
+    for s in range(2):
+        red_two.third_sum(s)
+        red_two.third_gather(s)
+    for s in range(2):
+        red_one.second_sum(s)
+        red_one.third_send(s)
+    dpre.times_wait()
+    dpre.windows(0)
+    dpre.windows(2)
+    dpre.outer(one_t, out_v)
+
+    def finish(g, _):
+        row = 4 * g
+        d_vol[pl.ds(row, 4)] = shifted(out_v, row).astype(BF16)
+        return 0
+
+    lax.fori_loop(0, 8, finish, 0)
+    for s in range(2):
+        red_two.second_gather(s)
+    for s in range(2):
+        red_one.third_sum(s)
+        red_one.third_gather(s)
+    for s in range(2):
+        red_two.first_gather(s)
+    for s in range(2):
+        red_one.second_gather(s)
+    for s in range(2):
+        red_two.pair_gather(s)
+    for s in range(2):
+        red_one.first_gather(s)
+    for s in range(2):
+        red_one.pair_gather(s)
+    for red in (red_two, red_one):
+        for s in range(2):
+            red.finish(s)
+            red.drain(s)
+    for field in (vol, cot, dpre):
+        field.drain()
 
 
 def from_slots(full, scale):
@@ -336,29 +540,7 @@
     return tiles.reshape(3, 3, 3, 128, 128)
 
 
-def all_sum(one, two, scale):
-    shape = jax.ShapeDtypeStruct((8, 32, 16, 128), BF16)
-    full_one, full_two = pl.pallas_call(
-        reduce_kernel,
-        out_shape=(shape, shape),
-        in_specs=[pl.BlockSpec(memory_space=pltpu.VMEM)] * 2,
-        out_specs=[pl.BlockSpec(memory_space=pltpu.VMEM)] * 2,
-        scratch_shapes=REDUCE_SCRATCH + REDUCE_SCRATCH,
-        compiler_params=pltpu.CompilerParams(collective_id=0, has_side_effects=True),
-    )(to_slots(one), to_slots(two))
-    return from_slots(full_one, scale), from_slots(full_two, scale)
-
-
 def body(volume, cotangent, kernel_one, kernel_two):
-    stacked = jnp.stack((volume, cotangent))
-    padded_both = padded_2(stacked, (("ta", 1), ("ha", 2), ("wa", 3)), 1)
-    volume_pad = padded_both[0]
-    cotangent_pad = padded_both[1]
-    pre = conv_local(volume_pad, kernel_one)
-    sig = jax.nn.sigmoid(pre)
-    hidden = (pre * sig).astype(jnp.bfloat16)
-    d_hidden = conv_local(cotangent_pad, flip_swap(kernel_two))
-    d_pre = (d_hidden * sig * (1.0 + pre * (1.0 - sig))).astype(jnp.bfloat16)
     total_cells = (
         volume.shape[0]
         * volume.shape[1]
@@ -368,12 +550,38 @@
         * lax.axis_size("wa")
     )
     scale = 1.0 / jnp.sqrt(jnp.float32(total_cells))
-    part_two = flip_swap(kernel_local(cotangent_pad, hidden))
-    d_pre_pad = padded_2(d_pre, (("ta", 0), ("ha", 1), ("wa", 2)), 1)
-    d_volume = conv_local(d_pre_pad, flip_swap(kernel_one)).astype(jnp.bfloat16)
-    part_one = kernel_local(volume_pad, d_pre)
-    grad_one, grad_two = all_sum(part_one, part_two, scale)
-    return (d_volume, grad_one, grad_two)
+    full = jax.ShapeDtypeStruct((8, 32, 16, 128), BF16)
+    taps = pltpu.VMEM((27, 128, 128), BF16)
+    d_volume, full_one, full_two = pl.pallas_call(
+        block_kernel,
+        out_shape=(jax.ShapeDtypeStruct((32, 16, 128), BF16), full, full),
+        in_specs=[pl.BlockSpec(memory_space=pl.ANY)] * 4,
+        out_specs=[pl.BlockSpec(memory_space=pltpu.VMEM)] * 3,
+        scratch_shapes=FIELD_SCRATCH * 3
+        + [pltpu.VMEM((8, 32, 16, 128), BF16)] * 2
+        + REDUCE_SCRATCH * 2
+        + [taps] * 4
+        + [pltpu.VMEM((34, 16, 384), F32)] * 2
+        + [
+            pltpu.VMEM((32, 16, 128), F32),
+            pltpu.VMEM((32, 16, 128), BF16),
+            pltpu.VMEM((128, 512), BF16),
+            pltpu.SemaphoreType.DMA((4,)),
+        ],
+        compiler_params=pltpu.CompilerParams(
+            collective_id=0, has_side_effects=True, vmem_limit_bytes=60 * 1024 * 1024
+        ),
+    )(
+        volume.reshape(32, 16, 128),
+        cotangent.reshape(32, 16, 128),
+        kernel_one.reshape(27, 128, 128),
+        kernel_two.reshape(27, 128, 128),
+    )
+    return (
+        d_volume.reshape(volume.shape),
+        from_slots(full_one, scale),
+        from_slots(full_two, scale),
+    )
 
 
 def solution(mesh):

time: 169 us -> 71.2 us (0.42)
  local copies, waits for them, and re-layouts: 41.5 us -> 5.72 us
  starting transfers between devices: 34.2 us -> 0 us
  matrix products: 23.3 us -> 0 us
  Pallas kernels: 47.1 us -> 64.3 us
  waiting for transfers between devices: 12.2 us -> 0 us
  other arithmetic: 7.31 us -> 0.32 us
    ppermute x12 -> x0, starting transfers between devices: 34.2 us -> none  [the longest x6 25.1 us: padded_2(): lax.ppermute(tail, axis, [(i, (i + 1) % count) for i in range(ends)])]
    dot_general x45 -> x0, matrix products: 23.3 us -> none  [the longest x18 12.9 us: kernel_local(): lax.dot_general(rows, right, (((0,), (0,)), ((), ())), preferred_element_...]
    pallas_call x1, Pallas kernels: 47.1 us -> 64.3 us  [body(): pl.pallas_call(block_kernel, out_shape=(jax.ShapeDtypeStruct((32, 16, 128...]
    reshape x19 -> x0, local copies, waits for them, and re-layouts: 15.3 us -> none  [the longest x18 13.3 us: window_rows(): return jnp.concatenate(pieces, axis=-1).reshape(-1, 3 * chans)]
    ppermute x12 -> x0, waiting for transfers between devices: 12.2 us -> none  [the longest x6 12.2 us: padded_2(): lax.ppermute(head, axis, [((i + 1) % count, i) for i in range(ends)])]
    unnamed x154 -> x5, local copies, waits for them, and re-layouts: 10.6 us -> 0.66 us
    slice x12 -> x0, local copies, waits for them, and re-layouts: 9.78 us -> none  [the longest x3 4.12 us: conv_local(): kernel[offset_t, offset_h].reshape(3 * chans, chans)]
    concatenate x20 -> x0, other arithmetic: 5.54 us -> none  [the longest x16 2.69 us: window_rows(): return jnp.concatenate(pieces, axis=-1).reshape(-1, 3 * chans)]
  transfers between devices with their start and end apart: 12 -> 0, of which waited for: 5 -> 0; matrix products, arithmetic and copies ran while one was open for 8% -> 0% of each run, Pallas kernels for 28% -> 0%
where the time goes in v2:
time: 71.2 us; the launch traced here: 71.1 us
  Pallas kernels  64.3 us (90%)
  local copies, waits for them, and re-layouts  5.72 us (8%)
    pallas_call x1, Pallas kernels, body(): pl.pallas_call(block_kernel, out_shape=(jax.ShapeDtypeStruct((32, 16, 128...  64.3 us
    mul x2, local copies, waits for them, and re-layouts, from_slots(): tiles = jnp.swapaxes(tiles, 0, 1).astype(F32) * scale  2.81 us
    slice x4, local copies, waits for them, and re-layouts, from_slots(): tiles = jnp.concatenate([full[:, :14], full[:, 16:29]], axis=1)  2.24 us

profile of v2, /device:TPU:1, one launch (start us, length us, event | category | flops | bytes accessed | tf_op | source)
XLA Modules:
  0.0 71.1 jit_solution(8017046857938510790)
XLA Ops:
  0.6 64.3 %shard_map.67 = (bf16[32,16,128]{2,1,0:T(8,128)(2,1)}, bf16[8,32,16,128]{3,2,1,0:T(8,128)(2,1)}, bf16[8,32,16,128]{3,2,1,0:T(8,128)(2,1)}) custom-call(bf16[32,16,128]{2,1,0:T(8,128)(2,1)} %bitcast.15, bf16[32,16,128]{2,1,0:T(8,128)(2,1)} %bitcast.16, bf16[27,128,128]{2,1,0:T(8,128)(2,1)} %bitcast.13, bf16[27,128,128]{2,1,0:T(8,128)(2,1)} %bitcast.14), custom_call_target="tpu_custom_call" | custom-call | tf_op jit(solution)/shard_map/pallas_call | solution.py:555
  65.0 0.0 copy-start
  65.0 1.1 %slice.13 = bf16[8,13,16,128]{3,2,1,0:T(8,128)(2,1)S(1)} slice(bf16[8,32,16,128]{3,2,1,0:T(8,128)(2,1)} %get-tuple-element.7), slice={[0:8], [16:29], [0:16], [0:128]} | slice | bytes 851968 | tf_op jit(solution)/shard_map/slice | solution.py:538
  66.1 1.1 %slice.12 = bf16[8,14,16,128]{3,2,1,0:T(8,128)(2,1)S(1)} slice(bf16[8,32,16,128]{3,2,1,0:T(8,128)(2,1)} %get-tuple-element.7), slice={[0:8], [0:14], [0:16], [0:128]} | slice | bytes 917504 | tf_op jit(solution)/shard_map/slice | solution.py:538
  67.2 0.0 copy-done
  67.3 0.2 multiply_bitcast_fusion
  67.4 1.4 %copy.8 = f32[27,8,16,128]{3,2,1,0:T(8,128)} copy(f32[27,8,16,128]{3,2,0,1:T(8,128)S(1)} %multiply_bitcast_fusion) | data formatting | bytes 3538944 | tf_op jit(solution)/shard_map/mul | solution.py:539
  68.8 0.2 multiply_bitcast_fusion.1
  69.0 0.0 copy-start.1
  69.0 1.4 %copy.7 = f32[27,8,16,128]{3,2,1,0:T(8,128)} copy(f32[27,8,16,128]{3,2,0,1:T(8,128)S(1)} %multiply_bitcast_fusion.1) | data formatting | bytes 3538944 | tf_op jit(solution)/shard_map/mul | solution.py:539
  70.4 0.0 copy-done.1
  70.4 0.7 copy.10
  (2 shorter events, 0.1 us)
Async XLA Ops:
  65.0 2.2 %copy-start = (bf16[8,32,16,128]{3,2,1,0:T(8,128)(2,1)S(1)}, bf16[8,32,16,128]{3,2,1,0:T(8,128)(2,1)}, u32[]{:S(2)}) copy-start(bf16[8,32,16,128]{3,2,1,0:T(8,128)(2,1)} %get-tuple-element.8) | copy-start | bytes 3145732
  69.0 1.4 %copy-start.1 = (bf16[32,16,128]{2,1,0:T(8,128)(2,1)S(1)}, bf16[32,16,128]{2,1,0:T(8,128)(2,1)}, u32[]{:S(2)}) copy-start(bf16[32,16,128]{2,1,0:T(8,128)(2,1)} %get-tuple-element.6) | copy-start | bytes 393220

commit v3 on v2

--- a/solution.py
+++ b/solution.py
@@ -1,5 +1,8 @@
+import functools
+
 import jax
 import jax.numpy as jnp
+import numpy as np
 from jax import lax
 from jax.experimental import pallas as pl
 from jax.experimental.pallas import tpu as pltpu
@@ -248,11 +251,12 @@
         self.go(2, self.ends_out.at[2], self.ends.at[1, 1], near(0, -1, 1))
         self.go(2, self.ends_out.at[3], self.ends.at[1, 0], near(0, 1, 1))
 
-    def bulk_send(self):
+    def bulk_send(self, half):
         near = self.at.near
-        own = self.raw.at[1, pl.ds(1, 32)]
-        self.go(3, own, self.raw.at[0, pl.ds(1, 32)], near(1, 0, 0))
-        self.go(3, own, self.raw.at[2, pl.ds(1, 32)], near(-1, 0, 0))
+        rows = pl.ds(1 + 16 * half, 16)
+        own = self.raw.at[1, rows]
+        self.go(3, own, self.raw.at[0, rows], near(1, 0, 0))
+        self.go(3, own, self.raw.at[2, rows], near(-1, 0, 0))
 
     def frame_wait(self):
         wait_bytes(self.raw.at[1, pl.ds(0, 2)], self.recvs.at[0])
@@ -408,22 +412,23 @@
     cot.stage()
     pl.semaphore_wait(barrier, len(others))
 
-    vol.bulk_send()
     vol.frame_send()
+    vol.bulk_send(0)
+    vol.bulk_send(1)
     cot.frame_send()
+    cot.bulk_send(0)
     loads[2].wait()
     transposed(two, two_t)
     loads[3].wait()
     vol.frame_wait()
     vol.rim_send()
-    cot.bulk_send()
-    vol.windows(1)
+    cot.bulk_send(1)
     cot.frame_wait()
     cot.rim_send()
+    vol.windows(1)
     cot.windows(1)
     vol.middle(one, out_v)
     cot.middle(two_t, out_c)
-    transposed(one, one_t)
 
     vol.times_wait()
     vol.windows(0)
@@ -465,9 +470,6 @@
     dpre.stage()
     dpre.frame_send()
     act_t[...] = dpre.raw[1, pl.ds(1, 32)].reshape(512, 128).T
-    for s in range(2):
-        red_two.pair_sum(s)
-        red_two.first_send(s)
     for t in range(3):
         for kh in range(3):
             rhs = vol.win[t, pl.ds(kh, 32)].reshape(512, 384)
@@ -477,29 +479,30 @@
                 block = got[:, 128 * kw : 128 * kw + 128].T.reshape(8, 16, 128)
                 part_one[:, slot_of(tap)] = block.astype(BF16)
     red_one.pair_send()
-    for s in range(2):
-        red_two.first_sum(s)
-        red_two.second_send(s)
-    for s in range(2):
-        red_one.pair_sum(s)
-        red_one.first_send(s)
+    grads = (red_two, red_one)
+    for red in grads:
+        for s in range(2):
+            red.pair_sum(s)
+            red.first_send(s)
     dpre.frame_wait()
-    dpre.bulk_send()
+    transposed(one, one_t)
+    dpre.windows(1)
+    dpre.middle(one_t, out_v)
+    for red in grads:
+        for s in range(2):
+            red.first_sum(s)
+            red.second_send(s)
+    dpre.bulk_send(0)
+    dpre.bulk_send(1)
     dpre.rim_send()
-    dpre.windows(1)
-    for s in range(2):
-        red_two.second_sum(s)
-        red_two.third_send(s)
-    dpre.middle(one_t, out_v)
-    for s in range(2):
-        red_one.first_sum(s)
-        red_one.second_send(s)
-    for s in range(2):
-        red_two.third_sum(s)
-        red_two.third_gather(s)
-    for s in range(2):
-        red_one.second_sum(s)
-        red_one.third_send(s)
+    for red in grads:
+        for s in range(2):
+            red.second_sum(s)
+            red.third_send(s)
+    for red in grads:
+        for s in range(2):
+            red.third_sum(s)
+            red.third_gather(s)
     dpre.times_wait()
     dpre.windows(0)
     dpre.windows(2)
@@ -511,22 +514,16 @@
         return 0
 
     lax.fori_loop(0, 8, finish, 0)
-    for s in range(2):
-        red_two.second_gather(s)
-    for s in range(2):
-        red_one.third_sum(s)
-        red_one.third_gather(s)
-    for s in range(2):
-        red_two.first_gather(s)
-    for s in range(2):
-        red_one.second_gather(s)
-    for s in range(2):
-        red_two.pair_gather(s)
-    for s in range(2):
-        red_one.first_gather(s)
-    for s in range(2):
-        red_one.pair_gather(s)
-    for red in (red_two, red_one):
+    for red in grads:
+        for s in range(2):
+            red.second_gather(s)
+    for red in grads:
+        for s in range(2):
+            red.first_gather(s)
+    for red in grads:
+        for s in range(2):
+            red.pair_gather(s)
+    for red in grads:
         for s in range(2):
             red.finish(s)
             red.drain(s)
@@ -534,10 +531,25 @@
         field.drain()
 
 
-def from_slots(full, scale):
-    tiles = jnp.concatenate([full[:, :14], full[:, 16:29]], axis=1)
-    tiles = jnp.swapaxes(tiles, 0, 1).astype(F32) * scale
-    return tiles.reshape(3, 3, 3, 128, 128)
+def scale_kernel(scale, full_one, full_two, d_in, grad_one, grad_two, d_out, buf, sems):
+    through = pltpu.make_async_copy(d_in, d_out, sems.at[2])
+    through.start()
+    for g, (full, grad) in enumerate(((full_two, grad_two), (full_one, grad_one))):
+
+        def step(tap, _):
+            tiles = full[:, tap + 2 * (tap // 14)].astype(F32) * scale
+            buf[g, tap] = tiles.reshape(128, 128)
+            pltpu.make_async_copy(buf.at[g, tap], grad.at[tap], sems.at[g]).start()
+            return 0
+
+        lax.fori_loop(0, 27, step, 0)
+    through.wait()
+    wait_bytes(buf.at[0], sems.at[0])
+    wait_bytes(buf.at[1], sems.at[1])
+
+
+def in_hbm(array):
+    return pltpu.with_memory_space_constraint(array, pltpu.HBM)
 
 
 def body(volume, cotangent, kernel_one, kernel_two):
@@ -549,13 +561,13 @@
         * lax.axis_size("ha")
         * lax.axis_size("wa")
     )
-    scale = 1.0 / jnp.sqrt(jnp.float32(total_cells))
+    scale = float(1.0 / np.sqrt(np.float32(total_cells)))
     full = jax.ShapeDtypeStruct((8, 32, 16, 128), BF16)
     taps = pltpu.VMEM((27, 128, 128), BF16)
     d_volume, full_one, full_two = pl.pallas_call(
         block_kernel,
         out_shape=(jax.ShapeDtypeStruct((32, 16, 128), BF16), full, full),
-        in_specs=[pl.BlockSpec(memory_space=pl.ANY)] * 4,
+        in_specs=[pl.BlockSpec(memory_space=pltpu.HBM)] * 4,
         out_specs=[pl.BlockSpec(memory_space=pltpu.VMEM)] * 3,
         scratch_shapes=FIELD_SCRATCH * 3
         + [pltpu.VMEM((8, 32, 16, 128), BF16)] * 2
@@ -569,18 +581,27 @@
             pltpu.SemaphoreType.DMA((4,)),
         ],
         compiler_params=pltpu.CompilerParams(
-            collective_id=0, has_side_effects=True, vmem_limit_bytes=60 * 1024 * 1024
+            collective_id=0, has_side_effects=True, vmem_limit_bytes=32 * 1024 * 1024
         ),
     )(
-        volume.reshape(32, 16, 128),
-        cotangent.reshape(32, 16, 128),
-        kernel_one.reshape(27, 128, 128),
-        kernel_two.reshape(27, 128, 128),
+        in_hbm(volume.reshape(32, 16, 128)),
+        in_hbm(cotangent.reshape(32, 16, 128)),
+        in_hbm(kernel_one.reshape(27, 128, 128)),
+        in_hbm(kernel_two.reshape(27, 128, 128)),
     )
+    grad = jax.ShapeDtypeStruct((27, 128, 128), F32)
+    grad_one, grad_two, d_volume = pl.pallas_call(
+        functools.partial(scale_kernel, scale),
+        out_shape=(grad, grad, jax.ShapeDtypeStruct((32, 16, 128), BF16)),
+        in_specs=[pl.BlockSpec(memory_space=pltpu.VMEM)] * 3,
+        out_specs=[pl.BlockSpec(memory_space=pl.ANY)] * 3,
+        scratch_shapes=[pltpu.VMEM((2, 27, 128, 128), F32), pltpu.SemaphoreType.DMA((3,))],
+        compiler_params=pltpu.CompilerParams(vmem_limit_bytes=16 * 1024 * 1024),
+    )(full_one, full_two, d_volume)
     return (
         d_volume.reshape(volume.shape),
-        from_slots(full_one, scale),
-        from_slots(full_two, scale),
+        grad_one.reshape(kernel_one.shape),
+        grad_two.reshape(kernel_two.shape),
     )
 
 

time: 71.2 us -> 59.4 us (0.83)
  local copies, waits for them, and re-layouts: 5.72 us -> 0 us
  Pallas kernels: 64.3 us -> 58.7 us
    pallas_call x1, Pallas kernels: 64.3 us -> 56.8 us  [body(): pl.pallas_call(block_kernel, out_shape=(jax.ShapeDtypeStruct((32, 16, 128...]
    mul x2 -> x0, local copies, waits for them, and re-layouts: 2.81 us -> none  [from_slots(): tiles = jnp.swapaxes(tiles, 0, 1).astype(F32) * scale]
    slice x4 -> x0, local copies, waits for them, and re-layouts: 2.24 us -> none  [from_slots(): tiles = jnp.concatenate([full[:, :14], full[:, 16:29]], axis=1)]
    pallas_call x0 -> x1, Pallas kernels: none -> 1.83 us  [body(): pl.pallas_call(functools.partial(scale_kernel, scale), out_shape=(grad, g...]
where the time goes in v3:
time: 59.4 us; the launch traced here: 59.3 us
  Pallas kernels  58.7 us (99%)
  between operations  0.64 us (1%)
    pallas_call x1, Pallas kernels, body(): pl.pallas_call(block_kernel, out_shape=(jax.ShapeDtypeStruct((32, 16, 128...  56.8 us
    pallas_call x1, Pallas kernels, body(): pl.pallas_call(functools.partial(scale_kernel, scale), out_shape=(grad, g...  1.83 us

profile of v3, /device:TPU:1, one launch (start us, length us, event | category | flops | bytes accessed | tf_op | source)
XLA Modules:
  0.0 59.3 jit_solution(3887779877950957804)
XLA Ops:
  0.6 56.8 %shard_map.67 = (bf16[32,16,128]{2,1,0:T(8,128)(2,1)S(1)}, bf16[8,32,16,128]{3,2,1,0:T(8,128)(2,1)S(1)}, bf16[8,32,16,128]{3,2,1,0:T(8,128)(2,1)S(1)}) custom-call(bf16[32,16,128]{2,1,0:T(8,128)(2,1)} %bitcast.9, bf16[32,16,128]{2,1,0:T(8,128)(2,1)} %bitcast.10, bf16[27,128,128]{2,1,0:T(8,128)(2,1)} %bitcast.7, bf16[27,128,128]{2,1,0:T(8,128)(2,1)} %bitcast.8), custom_call_target="tpu_custom_call" | custom-call | tf_op jit(solution)/shard_map/pallas_call | solution.py:567
  57.5 1.8 %shard_map.68 = (f32[27,128,128]{2,1,0:T(8,128)}, f32[27,128,128]{2,1,0:T(8,128)}, bf16[32,16,128]{2,1,0:T(8,128)(2,1)}) custom-call(bf16[8,32,16,128]{3,2,1,0:T(8,128)(2,1)S(1)} %get-tuple-element.9.full_one, bf16[8,32,16,128]{3,2,1,0:T(8,128)(2,1)S(1)} %get-tuple-element.10.full_two, bf16[32,16,128]{2,1,0:T(8,128)(2,1)S(1)} %get-tuple-element.11.d_in), custom_call_target="tpu_custom_call" | custom-call | tf_op jit(solution)/shard_map/pallas_call | solution.py:593

commit v4 on v3

--- a/solution.py
+++ b/solution.py
@@ -53,35 +53,33 @@
     pltpu.make_async_copy(ref, ref, sem).wait()
 
 
-PHASES = 8
+PHASES = 7
 
 
 class Reduce:
-    def __init__(self, place, part, full, land0, sums, land1, tops, land2, thirds, land3, lasts, sends, recvs):
+    def __init__(self, place, part, full, land0, sums, land1, tops, land2, thirds, sends, recvs):
         self.at = place
         self.part, self.full = part, full
         self.land0, self.sums, self.land1 = land0, sums, land1
-        self.tops, self.land2 = tops, land2
-        self.thirds, self.land3, self.lasts = thirds, land3, lasts
+        self.tops, self.land2, self.thirds = tops, land2, thirds
         self.sends, self.recvs = sends, recvs
 
     def first(self, s, off):
         return self.at.peer_x(off) if s == 0 else self.at.peer_y(off)
 
-    def second(self, s, off):
+    def last(self, s, off):
         return self.at.peer_y(off) if s == 0 else self.at.peer_x(off)
 
     def mine(self, s):
         return (self.at.x, self.at.y) if s == 0 else (self.at.y, self.at.x)
 
+    def go(self, phase, s, src, dst, device):
+        send(src, dst, self.sends.at[phase, s], self.recvs.at[phase, s], device)
+
     def pair_send(self):
         other = 4 - 4 * self.at.core
         for s in range(2):
-            send(
-                self.part.at[pl.ds(other, 4), pl.ds(16 * s, 14)],
-                self.land0.at[s],
-                self.sends.at[0, s], self.recvs.at[0, s], self.at.twin(),
-            )
+            self.go(0, s, self.part.at[pl.ds(other, 4), pl.ds(16 * s, 14)], self.land0.at[s], self.at.twin())
 
     def pair_sum(self, s):
         own = 4 * self.at.core
@@ -97,10 +95,7 @@
     def first_send(self, s):
         for off in range(1, 4):
             to, device = self.first(s, off)
-            send(
-                self.sums.at[s, to], self.land1.at[s, off - 1],
-                self.sends.at[1, s], self.recvs.at[1, s], device,
-            )
+            self.go(1, s, self.sums.at[s, to], self.land1.at[s, off - 1], device)
 
     def first_sum(self, s):
         me, _ = self.mine(s)
@@ -112,90 +107,68 @@
         self.tops[s, pl.ds(14, 2)] = jnp.zeros((2, 16, 128), BF16)
 
     def second_send(self, s):
-        for off in range(1, 4):
-            to, device = self.second(s, off)
-            send(
-                self.tops.at[s, pl.ds(4 * to, 4)], self.land2.at[s, off - 1],
-                self.sends.at[2, s], self.recvs.at[2, s], device,
-            )
+        for off in range(1, 8):
+            to, device = self.at.peer_z(off)
+            self.go(2, s, self.tops.at[s, pl.ds(2 * to, 2)], self.land2.at[s, off - 1], device)
 
     def second_sum(self, s):
         _, me = self.mine(s)
         wait_bytes(self.land2.at[s], self.recvs.at[2, s])
-        total = self.tops[s, pl.ds(4 * me, 4)].astype(F32)
-        for j in range(3):
+        total = self.tops[s, pl.ds(2 * self.at.z, 2)].astype(F32)
+        for j in range(7):
             total = total + self.land2[s, j].astype(F32)
-        self.thirds[s] = total.reshape(8, 8, 128)
+        self.thirds[s, me] = total.astype(BF16)
 
     def third_send(self, s):
-        for off in range(1, 8):
-            to, device = self.at.peer_z(off)
-            send(
-                self.thirds.at[s, to], self.land3.at[s, off - 1],
-                self.sends.at[3, s], self.recvs.at[3, s], device,
-            )
+        _, me = self.mine(s)
+        for off in range(1, 4):
+            _, device = self.last(s, off)
+            self.go(3, s, self.thirds.at[s, me], self.thirds.at[s, me], device)
+
+    def spot(self, s):
+        me, _ = self.mine(s)
+        return 4 * self.at.core + me, pl.ds(16 * s + 2 * self.at.z, 2)
 
     def third_sum(self, s):
-        wait_bytes(self.land3.at[s], self.recvs.at[3, s])
-        total = self.thirds[s, self.at.z]
-        for j in range(7):
-            total = total + self.land3[s, j]
-        self.lasts[s, self.at.z] = total
-
-    def third_gather(self, s):
+        wait_bytes(self.thirds.at[s, pl.ds(0, 3)], self.recvs.at[3, s])
+        total = self.thirds[s, 0].astype(F32)
+        for j in range(1, 4):
+            total = total + self.thirds[s, j].astype(F32)
+        row, slots = self.spot(s)
+        self.full[row, slots] = total.astype(BF16)
+
+    def second_gather(self, s):
+        row, slots = self.spot(s)
         for off in range(1, 8):
             _, device = self.at.peer_z(off)
-            send(
-                self.lasts.at[s, self.at.z], self.lasts.at[s, self.at.z],
-                self.sends.at[4, s], self.recvs.at[4, s], device,
-            )
-
-    def second_gather(self, s):
-        me, me2 = self.mine(s)
-        wait_bytes(self.lasts.at[s, pl.ds(0, 7)], self.recvs.at[4, s])
+            self.go(4, s, self.full.at[row, slots], self.full.at[row, slots], device)
+
+    def first_gather(self, s):
+        me, _ = self.mine(s)
+        wait_bytes(self.full.at[0, pl.ds(0, 14)], self.recvs.at[4, s])
         row = 4 * self.at.core + me
-        spot = pl.ds(16 * s + 4 * me2, 4)
-        self.full[row, spot] = self.lasts[s].reshape(4, 16, 128).astype(BF16)
-        for off in range(1, 4):
-            _, device = self.second(s, off)
-            send(
-                self.full.at[row, spot], self.full.at[row, spot],
-                self.sends.at[5, s], self.recvs.at[5, s], device,
-            )
-
-    def first_gather(self, s):
-        me, me2 = self.mine(s)
-        wait_bytes(self.full.at[0, pl.ds(0, 12)], self.recvs.at[5, s])
-        row = 4 * self.at.core + me
-        spot = pl.ds(16 * s, 14)
+        slots = pl.ds(16 * s, 14)
         for off in range(1, 4):
             _, device = self.first(s, off)
-            send(
-                self.full.at[row, spot], self.full.at[row, spot],
-                self.sends.at[6, s], self.recvs.at[6, s], device,
-            )
+            self.go(5, s, self.full.at[row, slots], self.full.at[row, slots], device)
 
     def pair_gather(self, s):
-        wait_bytes(self.full.at[pl.ds(0, 3), pl.ds(0, 14)], self.recvs.at[6, s])
+        wait_bytes(self.full.at[pl.ds(0, 3), pl.ds(0, 14)], self.recvs.at[5, s])
         rows = pl.ds(4 * self.at.core, 4)
-        spot = pl.ds(16 * s, 14)
-        send(
-            self.full.at[rows, spot], self.full.at[rows, spot],
-            self.sends.at[7, s], self.recvs.at[7, s], self.at.twin(),
-        )
+        slots = pl.ds(16 * s, 14)
+        self.go(6, s, self.full.at[rows, slots], self.full.at[rows, slots], self.at.twin())
 
     def finish(self, s):
-        wait_bytes(self.full.at[pl.ds(0, 4), pl.ds(0, 14)], self.recvs.at[7, s])
+        wait_bytes(self.full.at[pl.ds(0, 4), pl.ds(0, 14)], self.recvs.at[6, s])
 
     def drain(self, s):
         wait_bytes(self.land0.at[s], self.sends.at[0, s])
         wait_bytes(self.land1.at[s], self.sends.at[1, s])
         wait_bytes(self.land2.at[s], self.sends.at[2, s])
-        wait_bytes(self.land3.at[s], self.sends.at[3, s])
-        wait_bytes(self.lasts.at[s, pl.ds(0, 7)], self.sends.at[4, s])
-        wait_bytes(self.full.at[0, pl.ds(0, 12)], self.sends.at[5, s])
-        wait_bytes(self.full.at[pl.ds(0, 3), pl.ds(0, 14)], self.sends.at[6, s])
-        wait_bytes(self.full.at[pl.ds(0, 4), pl.ds(0, 14)], self.sends.at[7, s])
+        wait_bytes(self.thirds.at[s, pl.ds(0, 3)], self.sends.at[3, s])
+        wait_bytes(self.full.at[0, pl.ds(0, 14)], self.sends.at[4, s])
+        wait_bytes(self.full.at[pl.ds(0, 3), pl.ds(0, 14)], self.sends.at[5, s])
+        wait_bytes(self.full.at[pl.ds(0, 4), pl.ds(0, 14)], self.sends.at[6, s])
 
 
 REDUCE_SCRATCH = [
@@ -203,10 +176,8 @@
     pltpu.VMEM((2, 4, 14, 16, 128), BF16),
     pltpu.VMEM((2, 3, 14, 16, 128), BF16),
     pltpu.VMEM((2, 16, 16, 128), BF16),
-    pltpu.VMEM((2, 3, 4, 16, 128), BF16),
-    pltpu.VMEM((2, 8, 8, 128), F32),
-    pltpu.VMEM((2, 7, 8, 128), F32),
-    pltpu.VMEM((2, 8, 8, 128), F32),
+    pltpu.VMEM((2, 7, 2, 16, 128), BF16),
+    pltpu.VMEM((2, 4, 2, 16, 128), BF16),
     pltpu.SemaphoreType.DMA((PHASES, 2)),
     pltpu.SemaphoreType.DMA((PHASES, 2)),
 ]
@@ -502,7 +473,7 @@
     for red in grads:
         for s in range(2):
             red.third_sum(s)
-            red.third_gather(s)
+            red.second_gather(s)
     dpre.times_wait()
     dpre.windows(0)
     dpre.windows(2)
@@ -514,9 +485,6 @@
         return 0
 
     lax.fori_loop(0, 8, finish, 0)
-    for red in grads:
-        for s in range(2):
-            red.second_gather(s)
     for red in grads:
         for s in range(2):
             red.first_gather(s)

time: 59.4 us -> 57.8 us (0.973)
  Pallas kernels: 58.7 us -> 57 us
    pallas_call x1, Pallas kernels: 56.8 us -> 55.2 us  [body(): pl.pallas_call(block_kernel, out_shape=(jax.ShapeDtypeStruct((32, 16, 128...]
where the time goes in v4:
time: 57.8 us; the launch traced here: 57.7 us
  Pallas kernels  57 us (99%)
  between operations  0.64 us (1%)
    pallas_call x1, Pallas kernels, body(): pl.pallas_call(block_kernel, out_shape=(jax.ShapeDtypeStruct((32, 16, 128...  55.2 us
    pallas_call x1, Pallas kernels, body(): pl.pallas_call(functools.partial(scale_kernel, scale), out_shape=(grad, g...  1.83 us

profile of v4, /device:TPU:1, one launch (start us, length us, event | category | flops | bytes accessed | tf_op | source)
XLA Modules:
  0.0 57.7 jit_solution(16573817298654489896)
XLA Ops:
  0.6 55.2 %shard_map.67 = (bf16[32,16,128]{2,1,0:T(8,128)(2,1)S(1)}, bf16[8,32,16,128]{3,2,1,0:T(8,128)(2,1)S(1)}, bf16[8,32,16,128]{3,2,1,0:T(8,128)(2,1)S(1)}) custom-call(bf16[32,16,128]{2,1,0:T(8,128)(2,1)} %bitcast.9, bf16[32,16,128]{2,1,0:T(8,128)(2,1)} %bitcast.10, bf16[27,128,128]{2,1,0:T(8,128)(2,1)} %bitcast.7, bf16[27,128,128]{2,1,0:T(8,128)(2,1)} %bitcast.8), custom_call_target="tpu_custom_call" | custom-call | tf_op jit(solution)/shard_map/pallas_call | solution.py:535
  55.8 1.8 %shard_map.68 = (f32[27,128,128]{2,1,0:T(8,128)}, f32[27,128,128]{2,1,0:T(8,128)}, bf16[32,16,128]{2,1,0:T(8,128)(2,1)}) custom-call(bf16[8,32,16,128]{3,2,1,0:T(8,128)(2,1)S(1)} %get-tuple-element.9.full_one, bf16[8,32,16,128]{3,2,1,0:T(8,128)(2,1)S(1)} %get-tuple-element.10.full_two, bf16[32,16,128]{2,1,0:T(8,128)(2,1)S(1)} %get-tuple-element.11.d_in), custom_call_target="tpu_custom_call" | custom-call | tf_op jit(solution)/shard_map/pallas_call | solution.py:561

commit v5 on v4

--- a/solution.py
+++ b/solution.py
@@ -107,7 +107,7 @@
         self.tops[s, pl.ds(14, 2)] = jnp.zeros((2, 16, 128), BF16)
 
     def second_send(self, s):
-        for off in range(1, 8):
+        for off in (4, 3, 5, 2, 6, 1, 7):
             to, device = self.at.peer_z(off)
             self.go(2, s, self.tops.at[s, pl.ds(2 * to, 2)], self.land2.at[s, off - 1], device)
 
@@ -139,7 +139,7 @@
 
     def second_gather(self, s):
         row, slots = self.spot(s)
-        for off in range(1, 8):
+        for off in (4, 3, 5, 2, 6, 1, 7):
             _, device = self.at.peer_z(off)
             self.go(4, s, self.full.at[row, slots], self.full.at[row, slots], device)
 
@@ -441,6 +441,9 @@
     dpre.stage()
     dpre.frame_send()
     act_t[...] = dpre.raw[1, pl.ds(1, 32)].reshape(512, 128).T
+    for s in range(2):
+        red_two.pair_sum(s)
+        red_two.first_send(s)
     for t in range(3):
         for kh in range(3):
             rhs = vol.win[t, pl.ds(kh, 32)].reshape(512, 384)
@@ -451,10 +454,9 @@
                 part_one[:, slot_of(tap)] = block.astype(BF16)
     red_one.pair_send()
     grads = (red_two, red_one)
-    for red in grads:
-        for s in range(2):
-            red.pair_sum(s)
-            red.first_send(s)
+    for s in range(2):
+        red_one.pair_sum(s)
+        red_one.first_send(s)
     dpre.frame_wait()
     transposed(one, one_t)
     dpre.windows(1)

time: 57.8 us -> 56.8 us (0.983)
  Pallas kernels: 57 us -> 56.1 us
    pallas_call x1, Pallas kernels: 55.2 us -> 54.3 us  [body(): pl.pallas_call(block_kernel, out_shape=(jax.ShapeDtypeStruct((32, 16, 128...]
where the time goes in v5:
time: 56.8 us; the launch traced here: 56.7 us
  Pallas kernels  56.1 us (99%)
  between operations  0.64 us (1%)
    pallas_call x1, Pallas kernels, body(): pl.pallas_call(block_kernel, out_shape=(jax.ShapeDtypeStruct((32, 16, 128...  54.3 us
    pallas_call x1, Pallas kernels, body(): pl.pallas_call(functools.partial(scale_kernel, scale), out_shape=(grad, g...  1.83 us

profile of v5, /device:TPU:1, one launch (start us, length us, event | category | flops | bytes accessed | tf_op | source)
XLA Modules:
  0.0 56.7 jit_solution(3752019443802866269)
XLA Ops:
  0.6 54.3 %shard_map.67 = (bf16[32,16,128]{2,1,0:T(8,128)(2,1)S(1)}, bf16[8,32,16,128]{3,2,1,0:T(8,128)(2,1)S(1)}, bf16[8,32,16,128]{3,2,1,0:T(8,128)(2,1)S(1)}) custom-call(bf16[32,16,128]{2,1,0:T(8,128)(2,1)} %bitcast.9, bf16[32,16,128]{2,1,0:T(8,128)(2,1)} %bitcast.10, bf16[27,128,128]{2,1,0:T(8,128)(2,1)} %bitcast.7, bf16[27,128,128]{2,1,0:T(8,128)(2,1)} %bitcast.8), custom_call_target="tpu_custom_call" | custom-call | tf_op jit(solution)/shard_map/pallas_call | solution.py:537
  54.9 1.8 %shard_map.68 = (f32[27,128,128]{2,1,0:T(8,128)}, f32[27,128,128]{2,1,0:T(8,128)}, bf16[32,16,128]{2,1,0:T(8,128)(2,1)}) custom-call(bf16[8,32,16,128]{3,2,1,0:T(8,128)(2,1)S(1)} %get-tuple-element.9.full_one, bf16[8,32,16,128]{3,2,1,0:T(8,128)(2,1)S(1)} %get-tuple-element.10.full_two, bf16[32,16,128]{2,1,0:T(8,128)(2,1)S(1)} %get-tuple-element.11.d_in), custom_call_target="tpu_custom_call" | custom-call | tf_op jit(solution)/shard_map/pallas_call | solution.py:563

commit v6 on v5

--- a/solution.py
+++ b/solution.py
@@ -53,7 +53,8 @@
     pltpu.make_async_copy(ref, ref, sem).wait()
 
 
-PHASES = 7
+PHASES = 9
+ARRIVAL = {1: 5, 2: 7, 3: 8}
 
 
 class Reduce:
@@ -86,8 +87,7 @@
         wait_bytes(self.land0.at[s], self.recvs.at[0, s])
 
         def step(i, _):
-            total = self.part[own + i, pl.ds(16 * s, 14)].astype(F32) + self.land0[s, i].astype(F32)
-            self.sums[s, i] = total.astype(BF16)
+            self.sums[s, i] = self.part[own + i, pl.ds(16 * s, 14)] + self.land0[s, i]
             return 0
 
         lax.fori_loop(0, 4, step, 0)
@@ -147,16 +147,19 @@
         me, _ = self.mine(s)
         wait_bytes(self.full.at[0, pl.ds(0, 14)], self.recvs.at[4, s])
         row = 4 * self.at.core + me
-        slots = pl.ds(16 * s, 14)
+        own = self.full.at[row, pl.ds(16 * s, 14)]
         for off in range(1, 4):
             _, device = self.first(s, off)
-            self.go(5, s, self.full.at[row, slots], self.full.at[row, slots], device)
+            self.go(ARRIVAL[off], s, own, own, device)
+        self.go(6, s, own, own, self.at.twin())
 
     def pair_gather(self, s):
-        wait_bytes(self.full.at[pl.ds(0, 3), pl.ds(0, 14)], self.recvs.at[5, s])
-        rows = pl.ds(4 * self.at.core, 4)
-        slots = pl.ds(16 * s, 14)
-        self.go(6, s, self.full.at[rows, slots], self.full.at[rows, slots], self.at.twin())
+        me, _ = self.mine(s)
+        for off in (1, 3, 2):
+            wait_bytes(self.full.at[0, pl.ds(0, 14)], self.recvs.at[ARRIVAL[off], s])
+            row = 4 * self.at.core + lax.rem(me + 4 - off, 4)
+            got = self.full.at[row, pl.ds(16 * s, 14)]
+            self.go(6, s, got, got, self.at.twin())
 
     def finish(self, s):
         wait_bytes(self.full.at[pl.ds(0, 4), pl.ds(0, 14)], self.recvs.at[6, s])
@@ -167,7 +170,8 @@
         wait_bytes(self.land2.at[s], self.sends.at[2, s])
         wait_bytes(self.thirds.at[s, pl.ds(0, 3)], self.sends.at[3, s])
         wait_bytes(self.full.at[0, pl.ds(0, 14)], self.sends.at[4, s])
-        wait_bytes(self.full.at[pl.ds(0, 3), pl.ds(0, 14)], self.sends.at[5, s])
+        for phase in ARRIVAL.values():
+            wait_bytes(self.full.at[0, pl.ds(0, 14)], self.sends.at[phase, s])
         wait_bytes(self.full.at[pl.ds(0, 4), pl.ds(0, 14)], self.sends.at[6, s])
 
 
@@ -301,6 +305,10 @@
 
     def taps(self, weights, frame):
         rows = [weights[pl.ds(9 * frame + 3 * kh, 3)].reshape(384, 128) for kh in range(3)]
+        return jnp.concatenate(rows, axis=1)
+
+    def beside(self, frame):
+        rows = [self.win[frame, pl.ds(kh, 32)].reshape(512, 384) for kh in range(3)]
         return jnp.concatenate(rows, axis=1)
 
     def middle(self, weights, out):
@@ -384,9 +392,9 @@
     pl.semaphore_wait(barrier, len(others))
 
     vol.frame_send()
+    cot.frame_send()
     vol.bulk_send(0)
     vol.bulk_send(1)
-    cot.frame_send()
     cot.bulk_send(0)
     loads[2].wait()
     transposed(two, two_t)
@@ -417,17 +425,18 @@
     lax.fori_loop(0, 8, activate, 0)
     act_t[...] = act[...].reshape(512, 128).T
 
+    def two_taps(t):
+        got = jnp.dot(act_t[...], cot.beside(t), preferred_element_type=F32)
+        for n in range(9):
+            block = got[:, 128 * n : 128 * n + 128].reshape(8, 16, 128)
+            part_two[:, slot_of(26 - 9 * t - n)] = block.astype(BF16)
+
+    two_taps(1)
     cot.times_wait()
     cot.windows(0)
     cot.windows(2)
-    for t in range(3):
-        for kh in range(3):
-            rhs = cot.win[t, pl.ds(kh, 32)].reshape(512, 384)
-            got = jnp.dot(act_t[...], rhs, preferred_element_type=F32)
-            for kw in range(3):
-                tap = 26 - (9 * t + 3 * kh + kw)
-                block = got[:, 128 * kw : 128 * kw + 128].reshape(8, 16, 128)
-                part_two[:, slot_of(tap)] = block.astype(BF16)
+    for t in (0, 2):
+        two_taps(t)
     red_two.pair_send()
 
     cot.outer(two_t, out_c)
@@ -445,13 +454,10 @@
         red_two.pair_sum(s)
         red_two.first_send(s)
     for t in range(3):
-        for kh in range(3):
-            rhs = vol.win[t, pl.ds(kh, 32)].reshape(512, 384)
-            got = jnp.dot(act_t[...], rhs, preferred_element_type=F32)
-            for kw in range(3):
-                tap = 9 * t + 3 * kh + kw
-                block = got[:, 128 * kw : 128 * kw + 128].T.reshape(8, 16, 128)
-                part_one[:, slot_of(tap)] = block.astype(BF16)
+        got = jnp.dot(act_t[...], vol.beside(t), preferred_element_type=F32)
+        for n in range(9):
+            block = got[:, 128 * n : 128 * n + 128].T.reshape(8, 16, 128)
+            part_one[:, slot_of(9 * t + n)] = block.astype(BF16)
     red_one.pair_send()
     grads = (red_two, red_one)
     for s in range(2):
@@ -506,13 +512,15 @@
     through.start()
     for g, (full, grad) in enumerate(((full_two, grad_two), (full_one, grad_one))):
 
-        def step(tap, _):
-            tiles = full[:, tap + 2 * (tap // 14)].astype(F32) * scale
-            buf[g, tap] = tiles.reshape(128, 128)
-            pltpu.make_async_copy(buf.at[g, tap], grad.at[tap], sems.at[g]).start()
+        def step(i, _):
+            for tap in (3 * i, 3 * i + 1, 3 * i + 2):
+                tiles = full[:, tap + 2 * (tap // 14)].astype(F32) * scale
+                buf[g, tap] = tiles.reshape(128, 128)
+            three = pl.ds(3 * i, 3)
+            pltpu.make_async_copy(buf.at[g, three], grad.at[three], sems.at[g]).start()
             return 0
 
-        lax.fori_loop(0, 27, step, 0)
+        lax.fori_loop(0, 9, step, 0)
     through.wait()
     wait_bytes(buf.at[0], sems.at[0])
     wait_bytes(buf.at[1], sems.at[1])

time: 56.8 us -> 56.6 us (level)
  no operation moved by 1% of the time
where the time goes in v6:
time: 56.6 us; the launch traced here: 56.5 us
  Pallas kernels  55.8 us (99%)
  between operations  0.64 us (1%)
    pallas_call x1, Pallas kernels, body(): pl.pallas_call(block_kernel, out_shape=(jax.ShapeDtypeStruct((32, 16, 128...  54 us
    pallas_call x1, Pallas kernels, body(): pl.pallas_call(functools.partial(scale_kernel, scale), out_shape=(grad, g...  1.84 us

profile of v6, /device:TPU:1, one launch (start us, length us, event | category | flops | bytes accessed | tf_op | source)
XLA Modules:
  0.0 56.5 jit_solution(7482629955976999756)
XLA Ops:
  0.6 54.0 %shard_map.67 = (bf16[32,16,128]{2,1,0:T(8,128)(2,1)S(1)}, bf16[8,32,16,128]{3,2,1,0:T(8,128)(2,1)S(1)}, bf16[8,32,16,128]{3,2,1,0:T(8,128)(2,1)S(1)}) custom-call(bf16[32,16,128]{2,1,0:T(8,128)(2,1)} %bitcast.9, bf16[32,16,128]{2,1,0:T(8,128)(2,1)} %bitcast.10, bf16[27,128,128]{2,1,0:T(8,128)(2,1)} %bitcast.7, bf16[27,128,128]{2,1,0:T(8,128)(2,1)} %bitcast.8), custom_call_target="tpu_custom_call" | custom-call | tf_op jit(solution)/shard_map/pallas_call | solution.py:545
  54.6 1.8 %shard_map.68 = (f32[27,128,128]{2,1,0:T(8,128)}, f32[27,128,128]{2,1,0:T(8,128)}, bf16[32,16,128]{2,1,0:T(8,128)(2,1)}) custom-call(bf16[8,32,16,128]{3,2,1,0:T(8,128)(2,1)S(1)} %get-tuple-element.9.full_one, bf16[8,32,16,128]{3,2,1,0:T(8,128)(2,1)S(1)} %get-tuple-element.10.full_two, bf16[32,16,128]{2,1,0:T(8,128)(2,1)S(1)} %get-tuple-element.11.d_in), custom_call_target="tpu_custom_call" | custom-call | tf_op jit(solution)/shard_map/pallas_call | solution.py:571

commit v7 on v6

--- a/solution.py
+++ b/solution.py
@@ -482,6 +482,9 @@
         for s in range(2):
             red.third_sum(s)
             red.second_gather(s)
+    for red in grads:
+        for s in range(2):
+            red.first_gather(s)
     dpre.times_wait()
     dpre.windows(0)
     dpre.windows(2)
@@ -493,9 +496,6 @@
         return 0
 
     lax.fori_loop(0, 8, finish, 0)
-    for red in grads:
-        for s in range(2):
-            red.first_gather(s)
     for red in grads:
         for s in range(2):
             red.pair_gather(s)

time: 56.6 us -> 56.6 us (level)
  no operation moved by 1% of the time
where the time goes in v7:
time: 56.6 us; the launch traced here: 56.5 us
  Pallas kernels  55.8 us (99%)
  between operations  0.64 us (1%)
    pallas_call x1, Pallas kernels, body(): pl.pallas_call(block_kernel, out_shape=(jax.ShapeDtypeStruct((32, 16, 128...  54 us
    pallas_call x1, Pallas kernels, body(): pl.pallas_call(functools.partial(scale_kernel, scale), out_shape=(grad, g...  1.84 us

profile of v7, /device:TPU:1, one launch (start us, length us, event | category | flops | bytes accessed | tf_op | source)
XLA Modules:
  0.0 56.5 jit_solution(5569876676573450707)
XLA Ops:
  0.6 54.0 %shard_map.67 = (bf16[32,16,128]{2,1,0:T(8,128)(2,1)S(1)}, bf16[8,32,16,128]{3,2,1,0:T(8,128)(2,1)S(1)}, bf16[8,32,16,128]{3,2,1,0:T(8,128)(2,1)S(1)}) custom-call(bf16[32,16,128]{2,1,0:T(8,128)(2,1)} %bitcast.9, bf16[32,16,128]{2,1,0:T(8,128)(2,1)} %bitcast.10, bf16[27,128,128]{2,1,0:T(8,128)(2,1)} %bitcast.7, bf16[27,128,128]{2,1,0:T(8,128)(2,1)} %bitcast.8), custom_call_target="tpu_custom_call" | custom-call | tf_op jit(solution)/shard_map/pallas_call | solution.py:545
  54.6 1.8 %shard_map.68 = (f32[27,128,128]{2,1,0:T(8,128)}, f32[27,128,128]{2,1,0:T(8,128)}, bf16[32,16,128]{2,1,0:T(8,128)(2,1)}) custom-call(bf16[8,32,16,128]{3,2,1,0:T(8,128)(2,1)S(1)} %get-tuple-element.9.full_one, bf16[8,32,16,128]{3,2,1,0:T(8,128)(2,1)S(1)} %get-tuple-element.10.full_two, bf16[32,16,128]{2,1,0:T(8,128)(2,1)S(1)} %get-tuple-element.11.d_in), custom_call_target="tpu_custom_call" | custom-call | tf_op jit(solution)/shard_map/pallas_call | solution.py:571
